TPU v7x, 32 devices: a whole 2x2x4 slice. The times are simulated.
32 devices in a mesh: stage: 4 (over z), expert: 8 (over y, x, core).
Axes of the slice: x: 2, y: 2, z: 4, core: 2. Of those that a mesh axis runs over, the one named last changes fastest.
Arguments:
- tokens_in: bfloat16 [4, 8192, 1024], P('stage', 'expert')
- expert_ids: int32 [4, 8192, 8], P('stage', 'expert')
- gate_wts: float32 [4, 8192, 8], P('stage', 'expert')
- w_gate: bfloat16 [4, 32, 1024, 512], P('stage', 'expert')
- w_up: bfloat16 [4, 32, 1024, 512], P('stage', 'expert')
- w_down: bfloat16 [4, 32, 512, 1024], P('stage', 'expert')
- grad_out: bfloat16 [4, 8192, 1024], P('stage', 'expert')
Outputs:
- output 1: bfloat16 [4, 8192, 1024], P('stage', 'expert')
- output 2: bfloat16 [4, 8192, 1024], P('stage', 'expert')
- output 3: bfloat16 [4, 32, 1024, 512], P('stage', 'expert')
- output 4: bfloat16 [4, 32, 1024, 512], P('stage', 'expert')
- output 5: bfloat16 [4, 32, 512, 1024], P('stage', 'expert')
All inputs are finite; a program needn't handle non-finite values.
Results may differ from a plain program's by a relative error of at most 0.00782445.
Values are sent between devices in bfloat16 or wider.
A program may use at most 1 GiB of HBM per device.

v0:
```python
import jax
import jax.numpy as jnp
from jax import lax
from jax.sharding import PartitionSpec as P


def slot_table(rel_ids, n_local, capacity):
    is_held = (rel_ids >= 0) & (rel_ids < n_local)
    one_hot = (rel_ids[:, None] == jnp.arange(n_local, dtype=jnp.int32)[None, :]).astype(jnp.int32)
    slot_rank = jnp.sum((jnp.cumsum(one_hot, axis=0) - 1) * one_hot, axis=1)
    return jnp.where(is_held, rel_ids * capacity + slot_rank, n_local * capacity)


def row_table(slot_idx, capacity_rows):
    asg_count = slot_idx.shape[0]
    return jnp.full((capacity_rows,), asg_count, jnp.int32).at[slot_idx].set(jnp.arange(asg_count, dtype=jnp.int32), mode="drop")


def solution(mesh):
    n_stage = mesh.shape["stage"]
    n_group = mesh.shape["expert"]
    half_stage = n_stage // 2
    send_to_b = [(src_row, src_row + half_stage) for src_row in range(half_stage)]
    send_to_a = [(src_row + half_stage, src_row) for src_row in range(half_stage)]
    tok_spec = P("stage", "expert", None)
    w_spec = P("stage", "expert", None, None)

    def device_fn(tokens_in, expert_ids, gate_wts, w_gate, w_up, w_down, grad_out):
        tok_count, d_model = tokens_in.shape[1], tokens_in.shape[2]
        top_k = expert_ids.shape[2]
        local_count = w_gate.shape[1]
        n_experts = local_count * n_group
        capacity = 3 * tok_count * top_k // (2 * n_experts)
        buf_shape = (n_group, local_count, capacity, d_model)
        tokens = lax.ppermute(tokens_in[0], "stage", send_to_b)
        route_ids = lax.ppermute(expert_ids[0], "stage", send_to_b)
        gate_vals = lax.ppermute(gate_wts[0], "stage", send_to_b)
        asg_row = row_table(slot_table(route_ids.reshape(-1), n_experts, capacity), n_experts * capacity)
        tok_row = asg_row // top_k
        gate_row = jnp.concatenate([gate_vals.reshape(-1), jnp.zeros((1,), jnp.float32)])[asg_row]
        tok_pad = jnp.concatenate([tokens, jnp.zeros((1, d_model), tokens.dtype)], axis=0)
        recv_x = lax.all_to_all(tok_pad[tok_row].reshape(buf_shape), "expert", 0, 0, tiled=True)
        w_gate_loc = w_gate[0]
        w_up_loc = w_up[0]
        w_down_loc = w_down[0]
        pre_gate = jnp.einsum("secd,edf->secf", recv_x, w_gate_loc, preferred_element_type=jnp.float32)
        pre_up = jnp.einsum("secd,edf->secf", recv_x, w_up_loc, preferred_element_type=jnp.float32)
        sig_gate = jax.nn.sigmoid(pre_gate)
        act_gate = pre_gate * sig_gate
        hidden = (act_gate * pre_up).astype(jnp.bfloat16)
        out_rows = jnp.einsum("secf,efd->secd", hidden, w_down_loc, preferred_element_type=jnp.float32).astype(jnp.bfloat16)
        back_y = lax.all_to_all(out_rows, "expert", 0, 0, tiled=True).reshape(-1, d_model)
        y_sum = jax.ops.segment_sum(gate_row[:, None] * back_y.astype(jnp.float32), tok_row, num_segments=tok_count + 1)
        y_local = y_sum[:tok_count].astype(jnp.bfloat16)
        dy_pad = jnp.concatenate([grad_out[0], jnp.zeros((1, d_model), grad_out.dtype)], axis=0)
        send_g = (gate_row[:, None] * dy_pad[tok_row].astype(jnp.float32)).astype(jnp.bfloat16).reshape(buf_shape)
        recv_g = lax.all_to_all(send_g, "expert", 0, 0, tiled=True)
        d_hidden = jnp.einsum("secd,efd->secf", recv_g, w_down_loc, preferred_element_type=jnp.float32)
        d_gate = (d_hidden * pre_up * sig_gate * (1.0 + pre_gate * (1.0 - sig_gate))).astype(jnp.bfloat16)
        d_up = (d_hidden * act_gate).astype(jnp.bfloat16)
        dx_rows = (jnp.einsum("secf,edf->secd", d_gate, w_gate_loc, preferred_element_type=jnp.float32) + jnp.einsum("secf,edf->secd", d_up, w_up_loc, preferred_element_type=jnp.float32)).astype(jnp.bfloat16)
        back_dx = lax.all_to_all(dx_rows, "expert", 0, 0, tiled=True).reshape(-1, d_model)
        dx_sum = jax.ops.segment_sum(back_dx.astype(jnp.float32), tok_row, num_segments=tok_count + 1)
        dx_local = lax.ppermute(dx_sum[:tok_count].astype(jnp.bfloat16), "stage", send_to_a)
        grad_wg = jnp.einsum("secd,secf->edf", recv_x, d_gate, preferred_element_type=jnp.float32).astype(jnp.bfloat16)
        grad_wu = jnp.einsum("secd,secf->edf", recv_x, d_up, preferred_element_type=jnp.float32).astype(jnp.bfloat16)
        grad_wd = jnp.einsum("secf,secd->efd", hidden, recv_g, preferred_element_type=jnp.float32).astype(jnp.bfloat16)
        return y_local[None], dx_local[None], grad_wg[None], grad_wu[None], grad_wd[None]

    return jax.shard_map(device_fn, mesh=mesh, in_specs=(tok_spec, tok_spec, tok_spec, w_spec, w_spec, w_spec, tok_spec), out_specs=(tok_spec, tok_spec, w_spec, w_spec, w_spec), check_vma=False)
```

profile of v0, /device:TPU:25, one launch (start us, length us, event | category | flops | bytes accessed | tf_op | source)
XLA Modules:
  0.0 1590.4 jit_solution(13370332366523073105)
XLA Ops:
  11.0 17.1 %reduce-window.6 = s32[32,64,128]{2,1,0:T(8,128)S(1)} reduce-window(s32[32,64,128]{2,1,0:T(8,128)} %fusion.48, s32[]{:T(128)} %constant.12.clone.1), window={size=1x1x128 pad=0_0x0_0x127_0}, to_apply=%region_0.0 | reduce-window | flops 33292288 | bytes 2097156 | tf_op jit(solution)/shard_map/reduce-window
  30.5 30.5 %scatter_custom_fusion = s32[12288]{0:T(1024)S(1)} fusion(s32[8192]{0:T(1024)S(1)} %bitcast.130, s32[8192]{0:T(1024)S(1)} %iota.11, s32[]{:T(128)} %constant.16.clone.1), kind=kCustom, calls=%fused_computation.83 | custom fusion | bytes 49156 | tf_op jit(solution)/shard_map/scatter | solution.py:16
  61.6 68.0 %gather_fusion = f32[12288]{0:T(1024)S(1)} fusion(f32[8193]{0:T(1024)S(1)} %pad_maximum_fusion, s32[12288]{0:T(1024)S(1)} %get-tuple-element.8), kind=kCustom, calls=%fused_computation | custom fusion | bytes 147456 | tf_op jit(solution)/shard_map/gather | solution.py:40
  129.7 52.6 %gather_fusion.2 = bf16[12288,1024]{1,0:T(8,128)(2,1)} fusion(bf16[1025,1024]{1,0:T(8,128)(2,1)S(1)} %concatenate.11, s32[12288]{0:T(1024)S(1)} %get-tuple-element.9), kind=kCustom, calls=%fused_computation.2 | custom fusion | bytes 50380800 | tf_op jit(solution)/shard_map/gather | solution.py:56
  182.3 21.8 %fusion.2 = bf16[8,4,384,1024]{3,2,1,0:T(8,128)(2,1)} fusion(bf16[8,4,384,1024]{3,2,1,0:T(8,128)(2,1)} %bitcast.125, f32[8,4,384]{2,1,0:T(4,128)S(1)} %mul.67), kind=kLoop, calls=%fused_computation.9 | loop fusion | flops 37748736 | bytes 50380800 | tf_op jit(solution)/shard_map/convert_element_type | solution.py:56
  213.5 92.9 %collective-permute-done.2 = bf16[1024,1024]{1,0:T(8,128)(2,1)S(1)} collective-permute-done((bf16[1024,1024]{1,0:T(8,128)(2,1)S(1)}, bf16[1024,1024]{1,0:T(8,128)(2,1)S(1)}, u32[]{:S(2)}, u32[]{:S(2)}) %collective-permute-start.2) | collective-permute-done | bytes 2097184 | tf_op jit(solution)/shard_map/ppermute | solution.py:35
  306.6 52.6 %gather_fusion.1 = bf16[12288,1024]{1,0:T(8,128)(2,1)} fusion(bf16[1025,1024]{1,0:T(8,128)(2,1)S(1)} %concatenate.10, s32[12288]{0:T(1024)S(1)} %get-tuple-element.9), kind=kCustom, calls=%fused_computation.1 | custom fusion | bytes 50380800 | tf_op jit(solution)/shard_map/gather | solution.py:42
  359.2 123.4 %all-to-all-done.2 = bf16[8,4,384,1024]{3,2,1,0:T(8,128)(2,1)} async-done(((bf16[8,4,384,1024]{3,2,1,0:T(8,128)(2,1)}), bf16[8,4,384,1024]{3,2,1,0:T(8,128)(2,1)}, u32[]{:S(2)}, u32[]{:S(2)}) %all-to-all-start.2) | async-done | bytes 25165856 | tf_op jit(solution)/shard_map/all_to_all | solution.py:57
  493.1 25.6 %fusion.17 = f32[4,8,384,512]{3,2,1,0:T(8,128)} fusion(bf16[8,4,384,1024]{3,2,1,0:T(8,128)(2,1)} %all-to-all-done.2, bf16[1,4,512,1024]{3,2,1,0:T(8,128)(2,1)} %param.12), kind=kOutput, calls=%fused_computation.33 | convolution fusion | flops 12884901888 | bytes 54525952 | tf_op jit(solution)/shard_map/secd,efd->secf/dot_general | solution.py:58
  518.6 244.8 %all-to-all-done = bf16[8,4,384,1024]{3,2,1,0:T(8,128)(2,1)} async-done(((bf16[8,4,384,1024]{3,2,1,0:T(8,128)(2,1)}), bf16[8,4,384,1024]{3,2,1,0:T(8,128)(2,1)}, u32[]{:S(2)}, u32[]{:S(2)}) %all-to-all-start) | async-done | bytes 25165856 | tf_op jit(solution)/shard_map/all_to_all | solution.py:42
  763.4 25.7 %fusion.19 = f32[4,8,384,512]{3,2,1,0:T(8,128)} fusion(bf16[8,4,384,1024]{3,2,1,0:T(8,128)(2,1)} %all-to-all-done, bf16[1,4,1024,512]{3,2,1,0:T(8,128)(2,1)} %param.11), kind=kOutput, calls=%fused_computation.35 | convolution fusion | flops 12884901888 | bytes 54525952 | tf_op jit(solution)/shard_map/secd,edf->secf/dot_general | solution.py:47
  789.1 45.4 %fusion.8 = (bf16[8,4,384,512]{3,2,0,1:T(8,128)(2,1)}, bf16[8,4,384,512]{3,2,0,1:T(8,128)(2,1)}, bf16[8,4,384,512]{3,2,0,1:T(8,128)(2,1)}) fusion(f32[4,8,384,512]{3,2,1,0:T(8,128)} %fusion.17, f32[4,8,384,512]{3,2,1,0:T(8,128)} %fusion.19, bf16[1,4,1024,512]{3,2,1,0:T(8,128)(2,1)S(1)} %copy-done.2, bf16[8,4,384,1024]{3,2,1,0:T(8,128)(2,1)} %all-to-all-done), kind=kOutput, calls=%fused_computation.19 | convolution fusion | flops 12979273728 | bytes 117440512 | tf_op jit(solution)/shard_map/secd,edf->secf/dot_general | solution.py:46
  834.5 25.8 %fusion.32 = f32[4,8,384,1024]{3,2,1,0:T(8,128)} fusion(bf16[8,4,384,512]{3,2,0,1:T(8,128)(2,1)} %get-tuple-element.6, bf16[1,4,1024,512]{3,2,1,0:T(8,128)(2,1)} %param.10), kind=kOutput, calls=%fused_computation.53 | convolution fusion | flops 12884901888 | bytes 67108864 | tf_op jit(solution)/shard_map/secf,edf->secd/dot_general | solution.py:61
  860.4 33.4 %fusion.4 = bf16[8,4,384,1024]{3,2,0,1:T(8,128)(2,1)} fusion(f32[4,8,384,1024]{3,2,1,0:T(8,128)} %fusion.32, bf16[8,4,384,512]{3,2,0,1:T(8,128)(2,1)} %get-tuple-element.5, bf16[1,4,1024,512]{3,2,1,0:T(8,128)(2,1)} %param.11), kind=kOutput, calls=%fused_computation.13 | convolution fusion | flops 12910067712 | bytes 92274688 | tf_op jit(solution)/shard_map/secf,edf->secd/dot_general | solution.py:61
  893.8 20.6 %copy.37 = bf16[8,4,384,1024]{3,2,1,0:T(8,128)(2,1)} copy(bf16[8,4,384,1024]{3,2,0,1:T(8,128)(2,1)} %fusion.4) | data formatting | bytes 50331648 | tf_op jit(solution)/shard_map/convert_element_type | solution.py:61
  924.3 21.1 %convert_bitcast_fusion = bf16[8,4,384,1024]{3,2,0,1:T(8,128)(2,1)} fusion(bf16[8,4,384,512]{3,2,0,1:T(8,128)(2,1)} %get-tuple-element.7, bf16[1,4,512,1024]{3,2,1,0:T(8,128)(2,1)} %param.12), kind=kOutput, calls=%fused_computation.29 | convolution fusion | flops 12897484800 | bytes 41943040 | tf_op jit(solution)/shard_map/secf,efd->secd/dot_general | solution.py:51
  945.5 20.6 %copy.35 = bf16[8,4,384,1024]{3,2,1,0:T(8,128)(2,1)} copy(bf16[8,4,384,1024]{3,2,0,1:T(8,128)(2,1)} %convert_bitcast_fusion) | data formatting | bytes 50331648 | tf_op jit(solution)/shard_map/convert_element_type | solution.py:51
  966.1 228.6 %all-to-all-done.3 = bf16[8,4,384,1024]{3,2,1,0:T(8,128)(2,1)} async-done(((bf16[8,4,384,1024]{3,2,1,0:T(8,128)(2,1)}), bf16[8,4,384,1024]{3,2,1,0:T(8,128)(2,1)}, u32[]{:S(2)}, u32[]{:S(2)}) %all-to-all-start.3) | async-done | bytes 25165856 | tf_op jit(solution)/shard_map/all_to_all | solution.py:62
  1205.1 21.1 %fusion.29 = bf16[1,4,512,1024]{3,2,1,0:T(8,128)(2,1)} fusion(bf16[8,4,384,512]{3,2,0,1:T(8,128)(2,1)} %get-tuple-element.7, bf16[8,4,384,1024]{3,2,1,0:T(8,128)(2,1)} %all-to-all-done.2), kind=kOutput, calls=%fused_computation.48 | convolution fusion | flops 12886999040 | bytes 41943040 | tf_op jit(solution)/shard_map/secf,secd->efd/dot_general | solution.py:67
  1226.2 21.2 %fusion.28 = bf16[1,4,1024,512]{3,2,1,0:T(8,128)(2,1)} fusion(bf16[8,4,384,1024]{3,2,1,0:T(8,128)(2,1)} %all-to-all-done, bf16[8,4,384,512]{3,2,0,1:T(8,128)(2,1)} %get-tuple-element.5), kind=kOutput, calls=%fused_computation.47 | convolution fusion | flops 12886999040 | bytes 41943040 | tf_op jit(solution)/shard_map/secd,secf->edf/dot_general | solution.py:66
  1247.4 104.5 %scatter_custom_fusion.2 = f32[1025,1024]{1,0:T(8,128)} fusion(s32[12288]{0:T(1024)} %get-tuple-element.10, bf16[12288,1024]{1,0:T(8,128)(2,1)} %bitcast.39, f32[]{:T(128)} %constant.15.clone.1), kind=kCustom, calls=%fused_computation.6 | custom fusion | flops 25165824 | bytes 29364736 | tf_op jit(solution)/shard_map/scatter-add | solution.py:63
  1357.6 21.3 %fusion.27 = bf16[1,4,1024,512]{3,2,1,0:T(8,128)(2,1)} fusion(bf16[8,4,384,1024]{3,2,1,0:T(8,128)(2,1)} %all-to-all-done, bf16[8,4,384,512]{3,2,0,1:T(8,128)(2,1)} %get-tuple-element.6), kind=kOutput, calls=%fused_computation.46 | convolution fusion | flops 12886999040 | bytes 41943040 | tf_op jit(solution)/shard_map/secd,secf->edf/dot_general | solution.py:65
  1378.9 96.6 %all-to-all-done.1 = bf16[8,4,384,1024]{3,2,1,0:T(8,128)(2,1)} async-done(((bf16[8,4,384,1024]{3,2,1,0:T(8,128)(2,1)}), bf16[8,4,384,1024]{3,2,1,0:T(8,128)(2,1)}, u32[]{:S(2)}, u32[]{:S(2)}) %all-to-all-start.1) | async-done | bytes 25165856 | tf_op jit(solution)/shard_map/all_to_all | solution.py:52
  1475.5 107.6 %scatter_custom_fusion.1 = f32[1025,1024]{1,0:T(8,128)} fusion(s32[12288]{0:T(1024)} %get-tuple-element.10, bf16[12288,1024]{1,0:T(8,128)(2,1)} %bitcast.37, f32[12288]{0:T(1024)S(1)} %copy-done.1, f32[]{:T(128)} %constant.15.clone.1), kind=kCustom, calls=%fused_computation.11 | custom fusion | flops 37748736 | bytes 29413888 | tf_op jit(solution)/shard_map/scatter-add | solution.py:53
  (45 shorter events, 66.0 us)
Async XLA Ops:
  0.6 5.8 collective-permute-start
  1.9 7.0 collective-permute-start.1
  129.7 52.6 %copy-start = (f32[12288]{0:T(1024)}, f32[12288]{0:T(1024)S(1)}, u32[]{:S(2)}) copy-start(f32[12288]{0:T(1024)S(1)} %gather_fusion) | copy-start | bytes 147460
  204.1 8.1 copy-start.3
  204.1 278.5 %all-to-all-start.2 = ((bf16[8,4,384,1024]{3,2,1,0:T(8,128)(2,1)}), bf16[8,4,384,1024]{3,2,1,0:T(8,128)(2,1)}, u32[]{:S(2)}, u32[]{:S(2)}) async-start(bf16[8,4,384,1024]{3,2,1,0:T(8,128)(2,1)} %fusion.2), calls=%async_computation.2 | async-start | bytes 50331648 | tf_op jit(solution)/shard_map/all_to_all | solution.py:57
  212.2 94.2 %collective-permute-start.2 = (bf16[1024,1024]{1,0:T(8,128)(2,1)S(1)}, bf16[1024,1024]{1,0:T(8,128)(2,1)S(1)}, u32[]{:S(2)}, u32[]{:S(2)}) collective-permute-start(bf16[1024,1024]{1,0:T(8,128)(2,1)S(1)} %bitcast.131), channel_id=1, source_target_pairs={{0,16},{8,24},{1,17},{9,25},{2,18},{10,26},{3,19},{11,27},{4,20},{... | collective-permute-start | bytes 6291464 | tf_op jit(solution)/shard_map/ppermute | solution.py:35
  482.6 280.8 %all-to-all-start = ((bf16[8,4,384,1024]{3,2,1,0:T(8,128)(2,1)}), bf16[8,4,384,1024]{3,2,1,0:T(8,128)(2,1)}, u32[]{:S(2)}, u32[]{:S(2)}) async-start(bf16[8,4,384,1024]{3,2,1,0:T(8,128)(2,1)} %bitcast.124), calls=%async_computation | async-start | bytes 50331648 | tf_op jit(solution)/shard_map/all_to_all | solution.py:42
  763.4 25.7 %copy-start.2 = (bf16[1,4,1024,512]{3,2,1,0:T(8,128)(2,1)S(1)}, bf16[1,4,1024,512]{3,2,1,0:T(8,128)(2,1)}, u32[]{:S(2)}) copy-start(bf16[1,4,1024,512]{3,2,1,0:T(8,128)(2,1)} %param.10) | copy-start | bytes 12582916
  914.4 280.3 %all-to-all-start.3 = ((bf16[8,4,384,1024]{3,2,1,0:T(8,128)(2,1)}), bf16[8,4,384,1024]{3,2,1,0:T(8,128)(2,1)}, u32[]{:S(2)}, u32[]{:S(2)}) async-start(bf16[8,4,384,1024]{3,2,1,0:T(8,128)(2,1)} %copy.37), calls=%async_computation.3 | async-start | bytes 50331648 | tf_op jit(solution)/shard_map/all_to_all | solution.py:62
  1194.8 280.7 %all-to-all-start.1 = ((bf16[8,4,384,1024]{3,2,1,0:T(8,128)(2,1)}), bf16[8,4,384,1024]{3,2,1,0:T(8,128)(2,1)}, u32[]{:S(2)}, u32[]{:S(2)}) async-start(bf16[8,4,384,1024]{3,2,1,0:T(8,128)(2,1)} %copy.35), calls=%async_computation.1 | async-start | bytes 50331648 | tf_op jit(solution)/shard_map/all_to_all | solution.py:52
  1354.5 121.0 %copy-start.1 = (f32[12288]{0:T(1024)S(1)}, f32[12288]{0:T(1024)}, u32[]{:S(2)}) copy-start(f32[12288]{0:T(1024)} %copy-done) | copy-start | bytes 147460
  1354.5 232.4 %collective-permute-start.3 = (bf16[1024,1024]{1,0:T(8,128)(2,1)S(1)}, bf16[1024,1024]{1,0:T(8,128)(2,1)}, u32[]{:S(2)}, u32[]{:S(2)}) collective-permute-start(bf16[1024,1024]{1,0:T(8,128)(2,1)S(1)} %slice.33), channel_id=1, source_target_pairs={{16,0},{24,8},{17,1},{25,9},{18,2},{26,10},{19,3},{27,11},{20,4},{... | collective-permute-start | bytes 6291464 | tf_op jit(solution)/shard_map/ppermute | solution.py:64
where the time goes:
time: 1600 us; the launch traced here: 1590 us
  waiting for transfers between devices  789 us (49%)
  local copies, waits for them, and re-layouts  259 us (16%)
  other arithmetic  254 us (16%)
  matrix products  241 us (15%)
  starting transfers between devices  45.7 us (3%)
    all_to_all x1, waiting for transfers between devices, device_fn(): lax.all_to_all(tok_pad[tok_row].reshape(buf_shape), 'expert', 0, 0, tiled...  245 us
    all_to_all x1, waiting for transfers between devices, device_fn(): lax.all_to_all(dx_rows, 'expert', 0, 0, tiled=True).reshape(-1, d_model)  229 us
    all_to_all x1, waiting for transfers between devices, device_fn(): recv_g = lax.all_to_all(send_g, 'expert', 0, 0, tiled=True)  123 us
    scatter-add x1, other arithmetic, device_fn(): jax.ops.segment_sum(gate_row[:, None] * back_y.astype(jnp.float32), tok_r...  108 us
    scatter-add x1, other arithmetic, device_fn(): jax.ops.segment_sum(back_dx.astype(jnp.float32), tok_row, num_segments=to...  105 us
    all_to_all x1, waiting for transfers between devices, device_fn(): lax.all_to_all(out_rows, 'expert', 0, 0, tiled=True).reshape(-1, d_model)  96.6 us
    ppermute x1, waiting for transfers between devices, device_fn(): tokens = lax.ppermute(tokens_in[0], 'stage', send_to_b)  92.9 us
    gather x1, local copies, waits for them, and re-layouts, device_fn(): jnp.concatenate([gate_vals.reshape(-1), jnp.zeros((1,), jnp.float32)])  68 us
  transfers between devices with their start and end apart: 8, of which 7 were waited for; matrix products, arithmetic and copies ran while one was open for 25% of the time, Pallas kernels for 0%

commit v1 on v0

v1 whole, which is shorter than its diff:
```python
import functools

import jax
import jax.numpy as jnp
from jax import lax
from jax.experimental import pallas as pl
from jax.experimental.pallas import tpu as pltpu
from jax.sharding import PartitionSpec as P

MESH = pl.DeviceIdType.MESH
ANY = pl.BlockSpec(memory_space=pl.ANY)
F32 = jnp.float32
BF16 = jnp.bfloat16


def flip(ex, mask):
    bit_y = (ex // 4 + mask // 4) % 2
    bit_x = (ex // 2 + mask // 2) % 2
    bit_c = (ex + mask) % 2
    return bit_y * 4 + bit_x * 2 + bit_c


def dot(lhs, rhs, lhs_dim, rhs_dim):
    return lax.dot_general(lhs, rhs, (((lhs_dim,), (rhs_dim,)), ((), ())), preferred_element_type=F32)


AG_KINDS = (
    ((0, 1, 1), (0, 1, 1)),
    ((0, 2, 2), (0, 2, 2)),
    ((0, 4, 4), (0, 4, 4)),
    ((2, 1, 3), (2, 1, 3)),
    ((4, 1, 5), (4, 1, 5)),
    ((2, 4, 6), (4, 2, 6)),
    ((6, 1, 7), (6, 1, 7)),
)
K_OWN_P, K_OWN_X, K_OWN_Y, K_FWD_X, K_FWD_Y, K_DIAG, K_FWD_D = range(7)


def gather_kernel(n_half, x_ref, dy_ref, g_ref, xall, dyall, gall, own_buf, send_sem, recv_sem, z_send, z_recv, g_send, g_recv, loc_sem):
    st = lax.axis_index("stage")
    ex = lax.axis_index("expert")
    tok = x_ref.shape[0]
    rows_half = tok // 2
    bar = pltpu.get_barrier_semaphore()

    def block(arr, mask, half):
        start = pl.multiple_of(flip(ex, mask) * tok + half * rows_half, rows_half)
        return arr.at[pl.ds(start, rows_half)]

    def z_copy(half):
        return pltpu.make_async_remote_copy(
            src_ref=x_ref.at[pl.ds(half * rows_half, rows_half)], dst_ref=block(xall, 0, half),
            send_sem=z_send.at[half], recv_sem=z_recv.at[half], device_id=(st + n_half, ex), device_id_type=MESH)

    def zg_copy():
        return pltpu.make_async_remote_copy(
            src_ref=g_ref, dst_ref=gall.at[ex], send_sem=z_send.at[2], recv_sem=z_recv.at[2],
            device_id=(st + n_half, ex), device_id_type=MESH)

    @pl.when(st < n_half)
    def _():
        pl.semaphore_signal(bar, inc=1, device_id=(st + n_half, ex), device_id_type=MESH)
        pl.semaphore_wait(bar, 1)
        copies = [zg_copy(), z_copy(0), z_copy(1)]
        for c in copies:
            c.start()
        for c in copies:
            c.wait_send()

    @pl.when(st >= n_half)
    def _():
        pl.semaphore_signal(bar, inc=1, device_id=(st - n_half, ex), device_id_type=MESH)
        for mask in range(1, 8):
            pl.semaphore_signal(bar, inc=1, device_id=(st, flip(ex, mask)), device_id_type=MESH)
        pl.semaphore_wait(bar, 8)

        def copy(arr_id, kind, half, incoming=False):
            arr = (xall, dyall)[arr_id]
            sent, target, got = AG_KINDS[kind][half]
            sem = (arr_id * 7 + kind) * 2 + half
            dst = block(arr, got if incoming else sent, half)
            src = dst
            if sent == 0 and arr_id == 1 and not incoming:
                src = dy_ref.at[pl.ds(half * rows_half, rows_half)]
            return pltpu.make_async_remote_copy(
                src_ref=src, dst_ref=dst, send_sem=send_sem.at[sem], recv_sem=recv_sem.at[sem],
                device_id=(st, flip(ex, target)), device_id_type=MESH)

        def got(arr_id, kind, half):
            copy(arr_id, kind, half, incoming=True).wait_recv()

        def own(arr_id, half):
            for kind in (K_OWN_X, K_OWN_Y, K_OWN_P):
                copy(arr_id, kind, half).start()

        def relay(arr_id, half):
            got(arr_id, K_OWN_X, half)
            if half == 0:
                copy(arr_id, K_DIAG, 0).start()
            copy(arr_id, K_FWD_X, half).start()
            got(arr_id, K_OWN_Y, half)
            if half == 1:
                copy(arr_id, K_DIAG, 1).start()
            copy(arr_id, K_FWD_Y, half).start()

        def diag(arr_id, half):
            got(arr_id, K_DIAG, half)
            copy(arr_id, K_FWD_D, half).start()

        def g_copy(mask, incoming=False):
            idx = flip(ex, mask) if incoming else ex
            return pltpu.make_async_remote_copy(
                src_ref=gall.at[idx], dst_ref=gall.at[idx], send_sem=g_send.at[mask - 1], recv_sem=g_recv.at[mask - 1],
                device_id=(st, flip(ex, mask)), device_id_type=MESH)

        own(1, 0)
        own(1, 1)
        load = pltpu.make_async_copy(dy_ref, own_buf, loc_sem.at[0])
        load.start()
        load.wait()
        mine = dyall.at[pl.ds(pl.multiple_of(ex * tok, tok), tok)]
        save = pltpu.make_async_copy(own_buf, mine, loc_sem.at[1])
        save.start()
        pltpu.make_async_remote_copy(
            src_ref=gall.at[ex], dst_ref=gall.at[ex], send_sem=z_send.at[2], recv_sem=z_recv.at[2],
            device_id=(st - n_half, ex), device_id_type=MESH).wait_recv()
        for mask in range(1, 8):
            g_copy(mask).start()

        def x_arrived(half):
            blk = block(xall, 0, half)
            pltpu.make_async_remote_copy(
                src_ref=blk, dst_ref=blk, send_sem=z_send.at[half], recv_sem=z_recv.at[half],
                device_id=(st - n_half, ex), device_id_type=MESH).wait_recv()

        relay(1, 0)
        x_arrived(0)
        own(0, 0)
        relay(1, 1)
        diag(1, 0)
        diag(1, 1)
        relay(0, 0)
        x_arrived(1)
        own(0, 1)
        diag(0, 0)
        relay(0, 1)
        diag(0, 1)
        for arr_id in range(2):
            for half in range(2):
                for kind in (K_OWN_P, K_FWD_X, K_FWD_Y, K_FWD_D):
                    got(arr_id, kind, half)
        for mask in range(1, 8):
            g_copy(mask, incoming=True).wait_recv()
        for arr_id in range(2):
            for half in range(2):
                for kind in range(7):
                    copy(arr_id, kind, half).wait_send()
        for mask in range(1, 8):
            g_copy(mask).wait_send()
        save.wait()


def main_kernel(n_half, xall, dyall, gcol, w1, w3, w2, y_out, dx_out, dw1, dw3, dw2, hbuf, dabuf, dbbuf, sbuf, rbuf,
                w1v, w3v, w2v, xv, dyv, gv, acc, prv, hv, dav, dbv, tv, a1, a3, a2, o1, o3, o2, ov,
                w_sem, in_sem, st_sem, acc_sem, pr_sem, send_sem, recv_sem, t_sem, o_sem, dx_send, dx_recv, y_sem):
    st = lax.axis_index("stage")
    ex = lax.axis_index("expert")
    n_loc, d_model, d_ff = w1v.shape
    tile = xv.shape[1]
    tok = 2 * tile
    n_tiles = xall.shape[0] // tile
    bar = pltpu.get_barrier_semaphore()

    def dx_copy(half):
        return pltpu.make_async_remote_copy(
            src_ref=ov.at[half], dst_ref=dx_out.at[pl.ds(half * tile, tile)], send_sem=dx_send.at[half], recv_sem=dx_recv.at[half],
            device_id=(st - n_half, ex), device_id_type=MESH)

    @pl.when(st < n_half)
    def _():
        pl.semaphore_signal(bar, inc=1, device_id=(st + n_half, ex), device_id_type=MESH)
        pl.semaphore_wait(bar, 1)
        for half in range(2):
            view = dx_out.at[pl.ds(half * tile, tile)]
            pltpu.make_async_remote_copy(
                src_ref=view, dst_ref=view, send_sem=dx_send.at[half], recv_sem=dx_recv.at[half],
                device_id=(st + n_half, ex), device_id_type=MESH).wait_recv()

    @pl.when(st >= n_half)
    def _():
        pl.semaphore_signal(bar, inc=1, device_id=(st - n_half, ex), device_id_type=MESH)
        for mask in (1, 2, 4, 6):
            pl.semaphore_signal(bar, inc=1, device_id=(st, flip(ex, mask)), device_id_type=MESH)
        pl.semaphore_wait(bar, 5)

        w_loads = [pltpu.make_async_copy(a, b, w_sem.at[i]) for i, (a, b) in enumerate(((w1, w1v), (w3, w3v), (w2, w2v)))]
        for c in w_loads:
            c.start()

        def mask_of(k):
            return 7 - k // 2

        def row_of(k):
            return pl.multiple_of(flip(ex, mask_of(k)) * tok + (k % 2) * tile, tile)

        def x_loads(row, slot):
            rows = pl.ds(row, tile)
            return [pltpu.make_async_copy(xall.at[rows], xv.at[slot], in_sem.at[slot, 0]),
                    pltpu.make_async_copy(dyall.at[rows], dyv.at[slot], in_sem.at[slot, 1]),
                    pltpu.make_async_copy(gcol.at[rows], gv.at[slot], in_sem.at[slot, 2])]

        def gate_of(slot, e):
            g = gv[slot]
            lane = lax.broadcasted_iota(jnp.int32, g.shape, 1)
            return jnp.sum(jnp.where(lane == e, g, 0.0), axis=1, keepdims=True)

        def stores(row, e, slot):
            rows = pl.ds(row, tile)
            return [pltpu.make_async_copy(hv.at[slot], hbuf.at[e, rows], st_sem.at[slot, 0]),
                    pltpu.make_async_copy(dav.at[slot], dabuf.at[e, rows], st_sem.at[slot, 1]),
                    pltpu.make_async_copy(dbv.at[slot], dbbuf.at[e, rows], st_sem.at[slot, 2])]

        def slot_no(k):
            mask = mask_of(k)
            half = k % 2
            return jnp.where(mask % 2 == 1, (mask // 2) * 2 + half, 6 + (mask // 2) * 2 + half)

        def rs_copy(p, k):
            mask = mask_of(k)
            slot = slot_no(k)
            target = flip(ex, jnp.where(mask % 2 == 1, 1, mask))
            return pltpu.make_async_remote_copy(
                src_ref=sbuf.at[p, k], dst_ref=rbuf.at[p, slot], send_sem=send_sem.at[p, slot], recv_sem=recv_sem.at[p, slot],
                device_id=(st, target), device_id_type=MESH)

        def rs_arrived(p, slot):
            view = rbuf.at[p, slot]
            pltpu.make_async_remote_copy(
                src_ref=view, dst_ref=view, send_sem=send_sem.at[p, slot], recv_sem=recv_sem.at[p, slot],
                device_id=(st, flip(ex, 1)), device_id_type=MESH).wait_recv()

        def add_arrived(p, slot, dst):
            rs_arrived(p, slot)
            c = pltpu.make_async_copy(rbuf.at[p, slot], prv, pr_sem)
            c.start()
            c.wait()

            def add(i, _):
                rows = pl.ds(pl.multiple_of(i * 64, 64), 64)
                acc[dst, rows] = acc[dst, rows] + prv[rows]
                return 0
            lax.fori_loop(0, tile // 64, add, 0)

        def acc_save(p, k):
            return pltpu.make_async_copy(acc.at[k % 2], sbuf.at[p, k], acc_sem.at[k % 2])

        def finish_step(p, k):
            @pl.when(mask_of(k) % 2 == 0)
            def _():
                add_arrived(p, (mask_of(k) // 2) * 2 + k % 2, k % 2)
            acc_save(p, k).start()

        def send_previous(p, k):
            @pl.when(k > 0)
            def _():
                acc_save(p, k - 1).wait()

                @pl.when(mask_of(k - 1) > 0)
                def _():
                    rs_copy(p, k - 1).start()

        def finalize(p):
            for half in range(2):
                c = pltpu.make_async_copy(sbuf.at[p, 14 + half], acc.at[0], acc_sem.at[0])
                c.start()
                c.wait()
                for mask in (6, 4, 2):
                    add_arrived(p, 6 + mask + half, 0)
                ov[half] = acc[0].astype(BF16)

        for c in x_loads(row_of(0), 0):
            c.start()
        for c in w_loads:
            c.wait()

        def step_one(k, _):
            slot = k % 2
            row = row_of(k)

            @pl.when(k + 1 < n_tiles)
            def _():
                for c in x_loads(row_of(k + 1), (k + 1) % 2):
                    c.start()
            send_previous(0, k)
            for c in x_loads(row, slot):
                c.wait()
            acc[slot] = jnp.zeros(acc.shape[1:], F32)

            def expert(e, _):
                it = k * n_loc + e
                buf = it % 2

                @pl.when(it >= 2)
                def _():
                    for c in stores(row, e, buf):
                        c.wait()
                x = xv[slot]
                g = gate_of(slot, e)
                held = g > 0.0
                pre_gate = jnp.where(held, dot(x, w1v[e], 1, 0), 0.0)
                pre_up = jnp.where(held, dot(x, w3v[e], 1, 0), 0.0)
                sig = jax.nn.sigmoid(pre_gate)
                act = pre_gate * sig
                hv[buf] = (act * pre_up).astype(BF16)
                q = (g * dyv[slot].astype(F32)).astype(BF16)
                dh = dot(q, w2v[e], 1, 1)
                da = (dh * pre_up * sig * (1.0 + pre_gate * (1.0 - sig))).astype(BF16)
                db = (dh * act).astype(BF16)
                dav[buf] = da
                dbv[buf] = db
                c_rows = (dot(da, w1v[e], 1, 1) + dot(db, w3v[e], 1, 1)).astype(BF16)
                acc[slot] = acc[slot] + c_rows.astype(F32)
                for c in stores(row, e, buf):
                    c.start()
                return 0
            lax.fori_loop(0, n_loc, expert, 0)
            finish_step(0, k)
            return 0
        lax.fori_loop(0, n_tiles, step_one, 0)
        acc_save(0, n_tiles - 1).wait()
        for buf in range(2):
            for c in stores(0, 0, buf):
                c.wait()

        def h_loads(k):
            rows = pl.ds(row_of(k), tile)
            return [pltpu.make_async_copy(hbuf.at[e, rows], tv.at[k % 2, e], t_sem.at[k % 2, e]) for e in range(n_loc)] + [
                pltpu.make_async_copy(gcol.at[rows], gv.at[k % 2], in_sem.at[k % 2, 2])]

        for c in h_loads(0):
            c.start()

        def step_two(k, _):
            slot = k % 2

            @pl.when(k + 1 < n_tiles)
            def _():
                for c in h_loads(k + 1):
                    c.start()
            send_previous(1, k)
            for c in h_loads(k):
                c.wait()
            acc[slot] = jnp.zeros(acc.shape[1:], F32)

            def expert(e, _):
                out = dot(tv[slot, e], w2v[e], 1, 0).astype(BF16)
                acc[slot] = acc[slot] + gate_of(slot, e) * out.astype(F32)
                return 0
            lax.fori_loop(0, n_loc, expert, 0)
            finish_step(1, k)
            return 0
        lax.fori_loop(0, n_tiles, step_two, 0)
        acc_save(1, n_tiles - 1).wait()

        def d_loads(it):
            e = it // n_tiles
            slot = it % 2
            row = pl.multiple_of((it % n_tiles) * tile, tile)
            rows = pl.ds(row, tile)
            return x_loads(row, slot) + [
                pltpu.make_async_copy(hbuf.at[e, rows], tv.at[slot, 0], t_sem.at[slot, 0]),
                pltpu.make_async_copy(dabuf.at[e, rows], tv.at[slot, 1], t_sem.at[slot, 1]),
                pltpu.make_async_copy(dbbuf.at[e, rows], tv.at[slot, 2], t_sem.at[slot, 2])]

        def w_saves(e):
            return [pltpu.make_async_copy(o1, dw1.at[e], o_sem.at[0]), pltpu.make_async_copy(o3, dw3.at[e], o_sem.at[1]),
                    pltpu.make_async_copy(o2, dw2.at[e], o_sem.at[2])]

        for c in d_loads(0):
            c.start()
        total = n_loc * n_tiles

        def step_three(it, _):
            e = it // n_tiles
            slot = it % 2

            @pl.when(it + 1 < total)
            def _():
                for c in d_loads(it + 1):
                    c.start()

            @pl.when(it == n_tiles)
            def _():
                finalize(0)
                for half in range(2):
                    dx_copy(half).start()
            for c in d_loads(it):
                c.wait()

            @pl.when(it % n_tiles == 0)
            def _():
                a1[...] = jnp.zeros(a1.shape, F32)
                a3[...] = jnp.zeros(a3.shape, F32)
                a2[...] = jnp.zeros(a2.shape, F32)
            x = xv[slot]
            q = (gate_of(slot, e) * dyv[slot].astype(F32)).astype(BF16)
            a1[...] += dot(x, tv[slot, 1], 0, 0)
            a3[...] += dot(x, tv[slot, 2], 0, 0)
            a2[...] += dot(tv[slot, 0], q, 0, 0)

            @pl.when(it % n_tiles == n_tiles - 1)
            def _():
                @pl.when(e > 0)
                def _():
                    for c in w_saves(e):
                        c.wait()
                o1[...] = a1[...].astype(BF16)
                o3[...] = a3[...].astype(BF16)
                o2[...] = a2[...].astype(BF16)
                for c in w_saves(e):
                    c.start()
            return 0
        lax.fori_loop(0, total, step_three, 0)

        for half in range(2):
            dx_copy(half).wait_send()
        finalize(1)
        for half in range(2):
            c = pltpu.make_async_copy(ov.at[half], y_out.at[pl.ds(half * tile, tile)], y_sem.at[half])
            c.start()
        for half in range(2):
            pltpu.make_async_copy(ov.at[half], y_out.at[pl.ds(half * tile, tile)], y_sem.at[half]).wait()
        for c in w_saves(n_loc - 1):
            c.wait()

        def drain(k, _):
            rs_copy(0, k).wait_send()
            rs_copy(1, k).wait_send()
            return 0
        lax.fori_loop(0, n_tiles - 2, drain, 0)


def solution(mesh):
    n_stage = mesh.shape["stage"]
    n_group = mesh.shape["expert"]
    n_half = n_stage // 2
    tok_spec = P("stage", "expert", None)
    w_spec = P("stage", "expert", None, None)

    def device_fn(tokens_in, expert_ids, gate_wts, w_gate, w_up, w_down, grad_out):
        tok, d_model = tokens_in.shape[1:]
        n_loc, _, d_ff = w_gate.shape[1:]
        n_exp = n_loc * n_group
        lane = tok * n_group
        tile = tok // 2
        n_tiles = lane // tile
        is_b = lax.axis_index("stage") >= n_half
        ex = lax.axis_index("expert")
        ids = expert_ids[0].T[None]
        gate_t = jnp.sum(jnp.where(ids == jnp.arange(n_exp, dtype=jnp.int32)[:, None, None], gate_wts[0].T[None], 0.0), axis=1)

        sds = jax.ShapeDtypeStruct
        dma = pltpu.SemaphoreType.DMA
        xall, dyall, gall = pl.pallas_call(
            functools.partial(gather_kernel, n_half),
            out_shape=(sds((lane, d_model), BF16), sds((lane, d_model), BF16), sds((n_group, n_exp, tok), F32)),
            in_specs=[ANY] * 3,
            out_specs=(ANY,) * 3,
            scratch_shapes=[pltpu.VMEM((tok, d_model), BF16), dma((28,)), dma((28,)), dma((3,)), dma((3,)), dma((7,)), dma((7,)), dma((2,))],
            compiler_params=pltpu.CompilerParams(collective_id=0, has_side_effects=True),
            name="gather_tokens",
        )(tokens_in[0], grad_out[0], gate_t)
        gcol = lax.dynamic_slice_in_dim(gall, ex * n_loc, n_loc, axis=1).transpose(0, 2, 1).reshape(lane, n_loc)

        vm = pltpu.VMEM
        outs = pl.pallas_call(
            functools.partial(main_kernel, n_half),
            out_shape=(
                sds((tok, d_model), BF16), sds((tok, d_model), BF16),
                sds((n_loc, d_model, d_ff), BF16), sds((n_loc, d_model, d_ff), BF16), sds((n_loc, d_ff, d_model), BF16),
                sds((n_loc, lane, d_ff), BF16), sds((n_loc, lane, d_ff), BF16), sds((n_loc, lane, d_ff), BF16),
                sds((2, n_tiles, tile, d_model), F32), sds((2, n_tiles - 2, tile, d_model), F32)),
            in_specs=[ANY] * 6,
            out_specs=(ANY,) * 10,
            scratch_shapes=[
                vm((n_loc, d_model, d_ff), BF16), vm((n_loc, d_model, d_ff), BF16), vm((n_loc, d_ff, d_model), BF16),
                vm((2, tile, d_model), BF16), vm((2, tile, d_model), BF16), vm((2, tile, n_loc), F32),
                vm((2, tile, d_model), F32), vm((tile, d_model), F32),
                vm((2, tile, d_ff), BF16), vm((2, tile, d_ff), BF16), vm((2, tile, d_ff), BF16),
                vm((2, n_loc, tile, d_ff), BF16),
                vm((d_model, d_ff), F32), vm((d_model, d_ff), F32), vm((d_ff, d_model), F32),
                vm((d_model, d_ff), BF16), vm((d_model, d_ff), BF16), vm((d_ff, d_model), BF16),
                vm((2, tile, d_model), BF16),
                dma((3,)), dma((2, 3)), dma((2, 3)), dma((2,)), dma, dma((2, n_tiles - 2)), dma((2, n_tiles - 2)),
                dma((2, n_loc)), dma((3,)), dma((2,)), dma((2,)), dma((2,))],
            compiler_params=pltpu.CompilerParams(collective_id=1, has_side_effects=True, vmem_limit_bytes=63 * 1024 * 1024),
            name="experts",
        )(xall, dyall, gcol, w_gate[0], w_up[0], w_down[0])
        y_local, dx_local, grad_wg, grad_wu, grad_wd = outs[:5]
        on_b = [jnp.where(is_b, v, jnp.zeros_like(v))[None] for v in (y_local, grad_wg, grad_wu, grad_wd)]
        dx_local = jnp.where(is_b, jnp.zeros_like(dx_local), dx_local)
        return on_b[0], dx_local[None], on_b[1], on_b[2], on_b[3]

    return jax.shard_map(device_fn, mesh=mesh, in_specs=(tok_spec, tok_spec, tok_spec, w_spec, w_spec, w_spec, tok_spec), out_specs=(tok_spec, tok_spec, w_spec, w_spec, w_spec), check_vma=False)
```

time: 1600 us -> 724 us (0.45)
  waiting for transfers between devices: 789 us -> 0 us
  Pallas kernels: 0 us -> 703 us
  local copies, waits for them, and re-layouts: 259 us -> 6.24 us
  other arithmetic: 254 us -> 12.1 us
  matrix products: 241 us -> 0 us
  starting transfers between devices: 45.7 us -> 0 us
    pallas_call x0 -> x2, Pallas kernels: none -> 703 us  [the longest x1 507 us: device_fn(): pl.pallas_call(functools.partial(main_kernel, n_half), out_shape=(sds((to...]
    all_to_all x4 -> x0, waiting for transfers between devices: 693 us -> none  [the longest x1 245 us: device_fn(): lax.all_to_all(tok_pad[tok_row].reshape(buf_shape), 'expert', 0, 0, tiled...]
    dot_general x9 -> x0, matrix products: 241 us -> none  [the longest x1 45.4 us: device_fn(): jnp.einsum('secd,edf->secf', recv_x, w_gate_loc, preferred_element_type=j...]
    scatter-add x2 -> x0, other arithmetic: 212 us -> none  [the longest x1 108 us: device_fn(): jax.ops.segment_sum(gate_row[:, None] * back_y.astype(jnp.float32), tok_r...]
    gather x3 -> x0, local copies, waits for them, and re-layouts: 173 us -> none  [the longest x1 68 us: device_fn(): jnp.concatenate([gate_vals.reshape(-1), jnp.zeros((1,), jnp.float32)])]
    ppermute x4 -> x0, waiting for transfers between devices: 95.5 us -> none  [the longest x1 92.9 us: device_fn(): tokens = lax.ppermute(tokens_in[0], 'stage', send_to_b)]
    convert_element_type x2 -> x0, local copies, waits for them, and re-layouts: 41.3 us -> none  [the longest x1 20.6 us: device_fn(): jnp.einsum('secf,efd->secd', hidden, w_down_loc, preferred_element_type=j...]
    all_to_all x4 -> x0, starting transfers between devices: 38.7 us -> none  [the longest x1 10.4 us: device_fn(): lax.all_to_all(tok_pad[tok_row].reshape(buf_shape), 'expert', 0, 0, tiled...]
  transfers between devices with their start and end apart: 8 -> 0, of which waited for: 7 -> 0; matrix products, arithmetic and copies ran while one was open for 25% -> 0% of each run, Pallas kernels for 0% -> 0%
where the time goes in v1:
time: 724 us; the launch traced here: 722 us
  Pallas kernels  703 us (97%)
  other arithmetic  12.1 us (2%)
    pallas_call x1, Pallas kernels, device_fn(): pl.pallas_call(functools.partial(main_kernel, n_half), out_shape=(sds((to...  507 us
    pallas_call x1, Pallas kernels, device_fn(): pl.pallas_call(functools.partial(gather_kernel, n_half), out_shape=(sds((...  196 us

profile of v1, /device:TPU:25, one launch (start us, length us, event | category | flops | bytes accessed | tf_op | source)
XLA Modules:
  0.0 721.8 jit_solution(5974922648501338780)
XLA Ops:
  0.6 1.8 select_reduce_fusion.g_ref
  2.4 196.1 %gather_tokens.1 = (bf16[8192,1024]{1,0:T(8,128)(2,1)}, bf16[8192,1024]{1,0:T(8,128)(2,1)}, f32[8,32,1024]{2,1,0:T(8,128)}) custom-call(bf16[1024,1024]{1,0:T(8,128)(2,1)} %bitcast.28, bf16[1024,1024]{1,0:T(8,128)(2,1)} %bitcast.29, f32[32,1024]{1,0:T(8,128)} %select_reduce_fusion.g_ref), custom_call_target="tpu_custom_call" | custom-call | tf_op jit(solution)/shard_map/gather_tokens/pallas_call | solution.py:464
  198.5 1.0 dynamic-slice_bitcast_fusion
  199.5 2.7 copy.13
  202.2 506.6 %experts.1 = (bf16[1024,1024]{1,0:T(8,128)(2,1)}, bf16[1024,1024]{1,0:T(8,128)(2,1)}, bf16[4,1024,512]{2,1,0:T(8,128)(2,1)}, bf16[4,1024,512]{2,1,0:T(8,128)(2,1...) custom-call(bf16[8192,1024]{1,0:T(8,128)(2,1)} %get-tuple-element.13, ...), custom_call_target="tpu_custom_call" | custom-call | tf_op jit(solution)/shard_map/experts/pallas_call | solution.py:476
  708.9 0.0 copy-start.2
  708.9 4.0 select_bitcast_fusion.3
  712.9 0.0 copy-done.2
  712.9 0.0 copy-start
  712.9 0.0 copy-start.1
  712.9 2.4 select_bitcast_fusion
  715.3 1.3 copy-done
  716.6 1.3 copy-done.1
  717.9 3.9 select_bitcast_fusion.1
Async XLA Ops:
  708.9 4.1 copy-start.2
  712.9 3.7 copy-start
  712.9 5.0 copy-start.1

commit v2 on v1

v2 whole, which is shorter than its diff:
```python
import functools

import jax
import jax.numpy as jnp
from jax import lax
from jax.experimental import pallas as pl
from jax.experimental.pallas import tpu as pltpu
from jax.sharding import PartitionSpec as P

MESH = pl.DeviceIdType.MESH
ANY = pl.BlockSpec(memory_space=pl.ANY)
F32 = jnp.float32
BF16 = jnp.bfloat16


def flip(ex, mask):
    bit_y = (ex // 4 + mask // 4) % 2
    bit_x = (ex // 2 + mask // 2) % 2
    bit_c = (ex + mask) % 2
    return bit_y * 4 + bit_x * 2 + bit_c


def dot(lhs, rhs, lhs_dim, rhs_dim):
    return lax.dot_general(lhs, rhs, (((lhs_dim,), (rhs_dim,)), ((), ())), preferred_element_type=F32)


AG_KINDS = (
    ((0, 1, 1), (0, 1, 1)),
    ((0, 2, 2), (0, 2, 2)),
    ((0, 4, 4), (0, 4, 4)),
    ((2, 1, 3), (2, 1, 3)),
    ((4, 1, 5), (4, 1, 5)),
    ((2, 4, 6), (4, 2, 6)),
    ((6, 1, 7), (6, 1, 7)),
)
K_OWN_P, K_OWN_X, K_OWN_Y, K_FWD_X, K_FWD_Y, K_DIAG, K_FWD_D = range(7)


def gather_kernel(n_half, n_part, x_ref, dy_ref, g_ref, xall, dyall, gall, own_buf, send_sem, recv_sem, z_send, z_recv, g_send, g_recv, loc_sem):
    st = lax.axis_index("stage")
    ex = lax.axis_index("expert")
    tok = x_ref.shape[0]
    rows_half = tok // n_part
    bar = pltpu.get_barrier_semaphore()

    def block(arr, mask, half):
        start = pl.multiple_of(flip(ex, mask) * tok + half * rows_half, rows_half)
        return arr.at[pl.ds(start, rows_half)]

    def z_copy(half):
        return pltpu.make_async_remote_copy(
            src_ref=x_ref.at[pl.ds(half * rows_half, rows_half)], dst_ref=block(xall, 0, half),
            send_sem=z_send.at[half], recv_sem=z_recv.at[half], device_id=(st + n_half, ex), device_id_type=MESH)

    def zg_copy():
        return pltpu.make_async_remote_copy(
            src_ref=g_ref, dst_ref=gall.at[ex], send_sem=z_send.at[n_part], recv_sem=z_recv.at[n_part],
            device_id=(st + n_half, ex), device_id_type=MESH)

    @pl.when(st < n_half)
    def _():
        pl.semaphore_signal(bar, inc=1, device_id=(st + n_half, ex), device_id_type=MESH)
        pl.semaphore_wait(bar, 1)
        copies = [zg_copy()] + [z_copy(part) for part in range(n_part)]
        for c in copies:
            c.start()
        for c in copies:
            c.wait_send()

    @pl.when(st >= n_half)
    def _():
        pl.semaphore_signal(bar, inc=1, device_id=(st - n_half, ex), device_id_type=MESH)
        for mask in range(1, 8):
            pl.semaphore_signal(bar, inc=1, device_id=(st, flip(ex, mask)), device_id_type=MESH)
        pl.semaphore_wait(bar, 8)

        def copy(arr_id, kind, half, incoming=False):
            arr = (xall, dyall)[arr_id]
            sent, target, got = AG_KINDS[kind][half % 2]
            sem = (arr_id * 7 + kind) * n_part + half
            dst = block(arr, got if incoming else sent, half)
            src = dst
            if sent == 0 and arr_id == 1 and not incoming:
                src = dy_ref.at[pl.ds(half * rows_half, rows_half)]
            return pltpu.make_async_remote_copy(
                src_ref=src, dst_ref=dst, send_sem=send_sem.at[sem], recv_sem=recv_sem.at[sem],
                device_id=(st, flip(ex, target)), device_id_type=MESH)

        def got(arr_id, kind, half):
            copy(arr_id, kind, half, incoming=True).wait_recv()

        def own(arr_id, half):
            for kind in (K_OWN_X, K_OWN_Y, K_OWN_P):
                copy(arr_id, kind, half).start()

        def relay(arr_id, half):
            got(arr_id, K_OWN_X, half)
            if half % 2 == 0:
                copy(arr_id, K_DIAG, half).start()
            copy(arr_id, K_FWD_X, half).start()
            got(arr_id, K_OWN_Y, half)
            if half % 2 == 1:
                copy(arr_id, K_DIAG, half).start()
            copy(arr_id, K_FWD_Y, half).start()

        def diag(arr_id, half):
            got(arr_id, K_DIAG, half)
            copy(arr_id, K_FWD_D, half).start()

        def g_copy(mask, incoming=False):
            idx = flip(ex, mask) if incoming else ex
            return pltpu.make_async_remote_copy(
                src_ref=gall.at[idx], dst_ref=gall.at[idx], send_sem=g_send.at[mask - 1], recv_sem=g_recv.at[mask - 1],
                device_id=(st, flip(ex, mask)), device_id_type=MESH)

        for part in range(n_part):
            own(1, part)
        load = pltpu.make_async_copy(dy_ref, own_buf, loc_sem.at[0])
        load.start()
        load.wait()
        mine = dyall.at[pl.ds(pl.multiple_of(ex * tok, tok), tok)]
        save = pltpu.make_async_copy(own_buf, mine, loc_sem.at[1])
        save.start()
        pltpu.make_async_remote_copy(
            src_ref=gall.at[ex], dst_ref=gall.at[ex], send_sem=z_send.at[n_part], recv_sem=z_recv.at[n_part],
            device_id=(st - n_half, ex), device_id_type=MESH).wait_recv()
        for mask in range(1, 8):
            g_copy(mask).start()

        def x_arrived(half):
            blk = block(xall, 0, half)
            pltpu.make_async_remote_copy(
                src_ref=blk, dst_ref=blk, send_sem=z_send.at[half], recv_sem=z_recv.at[half],
                device_id=(st - n_half, ex), device_id_type=MESH).wait_recv()

        def own_x(part):
            x_arrived(part)
            own(0, part)

        plan = ((relay, 1, 0), (relay, 1, 1), (own_x, 0), (relay, 1, 2), (relay, 1, 3), (diag, 1, 0), (diag, 1, 1), (own_x, 1),
                (relay, 0, 0), (diag, 1, 2), (diag, 1, 3), (own_x, 2), (relay, 0, 1), (diag, 0, 0), (own_x, 3), (relay, 0, 2),
                (diag, 0, 1), (relay, 0, 3), (diag, 0, 2), (diag, 0, 3))
        for act, *where in plan:
            act(*where)
        for arr_id in range(2):
            for half in range(n_part):
                for kind in (K_OWN_P, K_FWD_X, K_FWD_Y, K_FWD_D):
                    got(arr_id, kind, half)
        for mask in range(1, 8):
            g_copy(mask, incoming=True).wait_recv()
        for arr_id in range(2):
            for half in range(n_part):
                for kind in range(7):
                    copy(arr_id, kind, half).wait_send()
        for mask in range(1, 8):
            g_copy(mask).wait_send()
        save.wait()


def main_kernel(n_half, cap, xall, dyall, mrow, mcol, w1, w3, w2, y_out, dx_out, dw1, dw3, dw2, xbuf, qbuf, hbuf, dabuf, dbbuf, sbuf, rbuf,
                w1v, w3v, w2v, xv, dyv, rv, cv, acc, prv, call, ptv, xs, qs, hs, tv, a1, a3, a2,
                w_sem, in_sem, st_sem, acc_sem, pr_sem, send_sem, recv_sem, t_sem, o_sem, dx_send, dx_recv, y_sem):
    st = lax.axis_index("stage")
    ex = lax.axis_index("expert")
    n_loc, d_model, d_ff = w1v.shape
    tok = xv.shape[1]
    tile = tok // 2
    n_blk = rv.shape[0]
    bar = pltpu.get_barrier_semaphore()

    def out_rows(half):
        return call.at[pl.ds(half * tile, tile)]

    def dx_copy(half):
        return pltpu.make_async_remote_copy(
            src_ref=out_rows(half), dst_ref=dx_out.at[pl.ds(half * tile, tile)], send_sem=dx_send.at[half], recv_sem=dx_recv.at[half],
            device_id=(st - n_half, ex), device_id_type=MESH)

    @pl.when(st < n_half)
    def _():
        pl.semaphore_signal(bar, inc=1, device_id=(st + n_half, ex), device_id_type=MESH)
        pl.semaphore_wait(bar, 1)
        for half in range(2):
            view = dx_out.at[pl.ds(half * tile, tile)]
            pltpu.make_async_remote_copy(
                src_ref=view, dst_ref=view, send_sem=dx_send.at[half], recv_sem=dx_recv.at[half],
                device_id=(st + n_half, ex), device_id_type=MESH).wait_recv()

    @pl.when(st >= n_half)
    def _():
        pl.semaphore_signal(bar, inc=1, device_id=(st - n_half, ex), device_id_type=MESH)
        for mask in (1, 2, 4):
            pl.semaphore_signal(bar, inc=1, device_id=(st, flip(ex, mask)), device_id_type=MESH)
        pl.semaphore_wait(bar, 4)

        w_loads = [pltpu.make_async_copy(a, b, w_sem.at[i])
                   for i, (a, b) in enumerate(((mrow, rv), (w1, w1v), (w3, w3v), (w2, w2v)))]
        for c in w_loads:
            c.start()

        def block_rows(k):
            return pl.ds(pl.multiple_of(flip(ex, 7 - k) * tok, tok), tok)

        def col_load(k):
            return pltpu.make_async_copy(mcol.at[block_rows(k)], cv.at[k % 2], in_sem.at[k % 2, 2])

        def x_loads(k):
            slot = k % 2
            return [pltpu.make_async_copy(xall.at[block_rows(k)], xv.at[slot], in_sem.at[slot, 0]),
                    pltpu.make_async_copy(dyall.at[block_rows(k)], dyv.at[slot], in_sem.at[slot, 1]), col_load(k)]

        def pick(slot, half, e):
            rank = cv[slot, half * tile:(half + 1) * tile, e:e + 1]
            return jnp.where(rank == lax.broadcasted_iota(jnp.int32, (tile, cap), 1).astype(F32), 1.0, 0.0).astype(BF16)

        def stores(k, e, buf):
            rows = pl.ds(pl.multiple_of(k * cap, cap), cap)
            mine = pl.ds(pl.multiple_of(buf * cap, cap), cap)
            pairs = [(xs.at[mine], xbuf), (qs.at[mine], qbuf)]
            for i, dst in enumerate((hbuf, dabuf, dbbuf)):
                pairs.append((hs.at[pl.ds(pl.multiple_of((buf * 3 + i) * cap, cap), cap)], dst))
            return [pltpu.make_async_copy(src, dst.at[e, rows], st_sem.at[buf, i]) for i, (src, dst) in enumerate(pairs)]

        def rs_copy(p, k, half):
            mask = 7 - k
            odd = mask % 2 == 1
            slot = jnp.where(odd, (mask // 2) * 2, 6 + mask) + half
            hop = jnp.where(odd, 1, jnp.where(mask == 6, 4 if half else 2, mask))
            return pltpu.make_async_remote_copy(
                src_ref=sbuf.at[p, k, half], dst_ref=rbuf.at[p, slot], send_sem=send_sem.at[p, slot], recv_sem=recv_sem.at[p, slot],
                device_id=(st, flip(ex, hop)), device_id_type=MESH)

        def add_arrived(p, slot, dst):
            view = rbuf.at[p, slot]
            pltpu.make_async_remote_copy(
                src_ref=view, dst_ref=view, send_sem=send_sem.at[p, slot], recv_sem=recv_sem.at[p, slot],
                device_id=(st, flip(ex, 1)), device_id_type=MESH).wait_recv()
            c = pltpu.make_async_copy(view, prv, pr_sem)
            c.start()
            c.wait()

            def add(i, _):
                rows = pl.ds(pl.multiple_of(i * 64, 64), 64)
                acc[dst, rows] = acc[dst, rows] + prv[rows]
                return 0
            lax.fori_loop(0, tile // 64, add, 0)

        def acc_save(p, k, half):
            return pltpu.make_async_copy(acc.at[half], sbuf.at[p, k, half], acc_sem.at[half])

        def finish(p, k, half):
            mask = 7 - k

            @pl.when(mask % 2 == 0)
            def _():
                add_arrived(p, (mask // 2) * 2 + half, half)
            if p == 0:
                @pl.when(mask == (2 if half else 4))
                def _():
                    add_arrived(p, 12 + half, half)
            acc_save(p, k, half).start()

        def send_previous(p, k):
            @pl.when(k > 0)
            def _():
                for half in range(2):
                    acc_save(p, k - 1, half).wait()
                    ready = k < n_blk if p == 0 else k != (6 if half else 4)

                    @pl.when(ready)
                    def _():
                        rs_copy(p, k - 1, half).start()

        def merge(half):
            k = 7 - (2 if half else 4)
            c = pltpu.make_async_copy(sbuf.at[1, k, half], acc.at[half], acc_sem.at[half])
            c.start()
            c.wait()
            add_arrived(1, 12 + half, half)
            acc_save(1, k, half).start()
            acc_save(1, k, half).wait()
            rs_copy(1, k, half).start()

        def finalize(p):
            for half in range(2):
                c = pltpu.make_async_copy(sbuf.at[p, 7, half], acc.at[half], acc_sem.at[half])
                c.start()
                c.wait()
                for mask in (4, 2):
                    add_arrived(p, 6 + mask + half, half)
                call[half * tile:(half + 1) * tile, :] = acc[half].astype(BF16)

        for c in x_loads(0):
            c.start()
        for c in w_loads:
            c.wait()

        def step_one(k, _):
            slot = k % 2
            blk = flip(ex, 7 - k)

            @pl.when(k + 1 < n_blk)
            def _():
                for c in x_loads(k + 1):
                    c.start()
            send_previous(0, k)
            for c in x_loads(k):
                c.wait()

            def expert(e, _):
                it = k * n_loc + e
                buf = it % 2

                @pl.when(it >= 2)
                def _():
                    for c in stores(k, e, buf):
                        c.wait()
                rank = rv[blk, pl.ds(e, 1), :]
                gate = rv[blk, pl.ds(e + n_loc, 1), :]
                held = rank == lax.broadcasted_iota(jnp.int32, (cap, tok), 0).astype(F32)
                take = jnp.where(held, 1.0, 0.0).astype(BF16)
                g = jnp.sum(jnp.where(held, gate, 0.0), axis=1, keepdims=True)
                x = dot(take, xv[slot], 1, 0).astype(BF16)
                q = (g * dot(take, dyv[slot], 1, 0)).astype(BF16)
                pre_gate = dot(x, w1v[e], 1, 0)
                pre_up = dot(x, w3v[e], 1, 0)
                dh = dot(q, w2v[e], 1, 1)
                sig = jax.nn.sigmoid(pre_gate)
                act = pre_gate * sig
                da = (dh * pre_up * sig * (1.0 + pre_gate * (1.0 - sig))).astype(BF16)
                db = (dh * act).astype(BF16)
                mine = pl.ds(pl.multiple_of(buf * cap, cap), cap)
                xs[mine, :] = x
                qs[mine, :] = q
                for i, val in enumerate(((act * pre_up).astype(BF16), da, db)):
                    hs[pl.ds(pl.multiple_of((buf * 3 + i) * cap, cap), cap), :] = val
                call[pl.ds(pl.multiple_of(e * cap, cap), cap), :] = (dot(da, w1v[e], 1, 1) + dot(db, w3v[e], 1, 1)).astype(BF16)
                for c in stores(k, e, buf):
                    c.start()
                return 0
            lax.fori_loop(0, n_loc, expert, 0)
            for half in range(2):
                for e in range(n_loc):
                    ptv[:, e * cap:(e + 1) * cap] = pick(slot, half, e)
                acc[half] = dot(ptv[...], call[...], 1, 0)
                finish(0, k, half)
            return 0
        lax.fori_loop(0, n_blk, step_one, 0)
        for half in range(2):
            acc_save(0, n_blk - 1, half).wait()
        for buf in range(2):
            for c in stores(0, 0, buf):
                c.wait()

        def h_loads(k):
            rows = pl.ds(pl.multiple_of(k * cap, cap), cap)
            return [pltpu.make_async_copy(hbuf.at[e, rows], tv.at[k % 2, pl.ds(e * cap, cap)], t_sem.at[k % 2, e])
                    for e in range(n_loc)] + [col_load(k)]

        for c in h_loads(0):
            c.start()

        def step_two(k, _):
            slot = k % 2

            @pl.when(k + 1 < n_blk)
            def _():
                for c in h_loads(k + 1):
                    c.start()
            send_previous(1, k)
            for c in h_loads(k):
                c.wait()
            for e in range(n_loc):
                out = dot(tv[slot, e * cap:(e + 1) * cap, :], w2v[e], 1, 0).astype(BF16)
                for half in range(2):
                    gate = cv[slot, half * tile:(half + 1) * tile, n_loc + e:n_loc + e + 1]
                    part = gate * dot(pick(slot, half, e), out, 1, 0)
                    acc[half] = part if e == 0 else acc[half] + part
            for half in range(2):
                finish(1, k, half)
            return 0
        lax.fori_loop(0, n_blk, step_two, 0)
        for half in range(2):
            acc_save(1, n_blk - 1, half).wait()

        depth = 2 * cap
        per_e = n_blk // 2

        def d_loads(it):
            e = it // per_e
            slot = it % 2
            rows = pl.ds(pl.multiple_of((it % per_e) * depth, depth), depth)
            top = pl.ds(0, depth)
            return [pltpu.make_async_copy(xbuf.at[e, rows], xv.at[slot, top], in_sem.at[slot, 0]),
                    pltpu.make_async_copy(qbuf.at[e, rows], dyv.at[slot, top], in_sem.at[slot, 1])] + [
                pltpu.make_async_copy(src.at[e, rows], tv.at[slot, pl.ds(i * depth, depth)], t_sem.at[slot, i])
                for i, src in enumerate((hbuf, dabuf, dbbuf))]

        def w_saves(e):
            return [pltpu.make_async_copy(hs.at[pl.ds(0, d_model)], dw1.at[e], o_sem.at[0]),
                    pltpu.make_async_copy(hs.at[pl.ds(d_model, d_model)], dw3.at[e], o_sem.at[1]),
                    pltpu.make_async_copy(qs.at[pl.ds(0, d_ff)], dw2.at[e], o_sem.at[2])]

        for c in d_loads(0):
            c.start()
        total = n_loc * per_e

        def step_three(it, _):
            e = it // per_e
            slot = it % 2

            @pl.when(it + 1 < total)
            def _():
                for c in d_loads(it + 1):
                    c.start()

            @pl.when(it == 2)
            def _():
                finalize(0)
                for half in range(2):
                    dx_copy(half).start()

            @pl.when(it == 8)
            def _():
                merge(1)

            @pl.when(it == 12)
            def _():
                merge(0)
            for c in d_loads(it):
                c.wait()

            @pl.when(it % per_e == 0)
            def _():
                a1[...] = jnp.zeros(a1.shape, F32)
                a3[...] = jnp.zeros(a3.shape, F32)
                a2[...] = jnp.zeros(a2.shape, F32)
            x = xv[slot, 0:depth, :]
            a1[...] += dot(x, tv[slot, depth:2 * depth, :], 0, 0)
            a3[...] += dot(x, tv[slot, 2 * depth:3 * depth, :], 0, 0)
            a2[...] += dot(tv[slot, 0:depth, :], dyv[slot, 0:depth, :], 0, 0)

            @pl.when(it % per_e == per_e - 1)
            def _():
                @pl.when(e > 0)
                def _():
                    for c in w_saves(e):
                        c.wait()
                hs[0:d_model, :] = a1[...].astype(BF16)
                hs[d_model:2 * d_model, :] = a3[...].astype(BF16)
                qs[0:d_ff, :] = a2[...].astype(BF16)
                for c in w_saves(e):
                    c.start()
            return 0
        lax.fori_loop(0, total, step_three, 0)

        for half in range(2):
            dx_copy(half).wait_send()
        finalize(1)

        def y_save(half):
            return pltpu.make_async_copy(out_rows(half), y_out.at[pl.ds(half * tile, tile)], y_sem.at[half])
        for half in range(2):
            y_save(half).start()
        for half in range(2):
            y_save(half).wait()
        for c in w_saves(n_loc - 1):
            c.wait()

        def drain(k, _):
            for p in range(2):
                for half in range(2):
                    rs_copy(p, k, half).wait_send()
            return 0
        lax.fori_loop(0, n_blk - 1, drain, 0)


def solution(mesh):
    n_stage = mesh.shape["stage"]
    n_group = mesh.shape["expert"]
    n_half = n_stage // 2
    tok_spec = P("stage", "expert", None)
    w_spec = P("stage", "expert", None, None)

    def device_fn(tokens_in, expert_ids, gate_wts, w_gate, w_up, w_down, grad_out):
        tok, d_model = tokens_in.shape[1:]
        n_loc, _, d_ff = w_gate.shape[1:]
        n_exp = n_loc * n_group
        lane = tok * n_group
        tile = tok // 2
        top_k = expert_ids.shape[2]
        cap = 3 * tok * top_k // (2 * n_exp)
        n_part = 4
        is_b = lax.axis_index("stage") >= n_half
        ex = lax.axis_index("expert")
        ids = expert_ids[0].T[None]
        gate_t = jnp.sum(jnp.where(ids == jnp.arange(n_exp, dtype=jnp.int32)[:, None, None], gate_wts[0].T[None], 0.0), axis=1)

        sds = jax.ShapeDtypeStruct
        dma = pltpu.SemaphoreType.DMA
        xall, dyall, gall = pl.pallas_call(
            functools.partial(gather_kernel, n_half, n_part),
            out_shape=(sds((lane, d_model), BF16), sds((lane, d_model), BF16), sds((n_group, n_exp, tok), F32)),
            in_specs=[ANY] * 3,
            out_specs=(ANY,) * 3,
            scratch_shapes=[pltpu.VMEM((tok, d_model), BF16), dma((14 * n_part,)), dma((14 * n_part,)), dma((n_part + 1,)), dma((n_part + 1,)), dma((7,)), dma((7,)), dma((2,))],
            compiler_params=pltpu.CompilerParams(collective_id=0, has_side_effects=True),
            name="gather_tokens",
        )(tokens_in[0], grad_out[0], gate_t)
        gate_row = lax.dynamic_slice_in_dim(gall, ex * n_loc, n_loc, axis=1)
        held = gate_row > 0.0
        upper = (jnp.arange(tok)[:, None] <= jnp.arange(tok)[None, :]).astype(BF16)
        count = jnp.einsum("set,tu->seu", held.astype(BF16), upper, preferred_element_type=F32)
        mrow = jnp.concatenate([jnp.where(held, count - 1.0, -1.0), gate_row], axis=1)
        mcol = mrow.transpose(0, 2, 1).reshape(lane, 2 * n_loc)

        vm = pltpu.VMEM
        rows = n_group * cap
        outs = pl.pallas_call(
            functools.partial(main_kernel, n_half, cap),
            out_shape=(
                sds((tok, d_model), BF16), sds((tok, d_model), BF16),
                sds((n_loc, d_model, d_ff), BF16), sds((n_loc, d_model, d_ff), BF16), sds((n_loc, d_ff, d_model), BF16),
                sds((n_loc, rows, d_model), BF16), sds((n_loc, rows, d_model), BF16),
                sds((n_loc, rows, d_ff), BF16), sds((n_loc, rows, d_ff), BF16), sds((n_loc, rows, d_ff), BF16),
                sds((2, n_group, 2, tile, d_model), F32), sds((2, 14, tile, d_model), F32)),
            in_specs=[ANY] * 7,
            out_specs=(ANY,) * 12,
            scratch_shapes=[
                vm((n_loc, d_model, d_ff), BF16), vm((n_loc, d_model, d_ff), BF16), vm((n_loc, d_ff, d_model), BF16),
                vm((2, tok, d_model), BF16), vm((2, tok, d_model), BF16), vm((n_group, 2 * n_loc, tok), F32), vm((2, tok, 2 * n_loc), F32),
                vm((2, tile, d_model), F32), vm((tile, d_model), F32), vm((n_loc * cap, d_model), BF16), vm((tile, n_loc * cap), BF16),
                vm((2 * cap, d_model), BF16), vm((2 * cap, d_model), BF16), vm((6 * cap, d_ff), BF16), vm((2, 6 * cap, d_ff), BF16),
                vm((d_model, d_ff), F32), vm((d_model, d_ff), F32), vm((d_ff, d_model), F32),
                dma((4,)), dma((2, 3)), dma((2, 5)), dma((2,)), dma, dma((2, 14)), dma((2, 14)),
                dma((2, n_loc)), dma((3,)), dma((2,)), dma((2,)), dma((2,))],
            compiler_params=pltpu.CompilerParams(collective_id=1, has_side_effects=True, vmem_limit_bytes=63 * 1024 * 1024),
            name="experts",
        )(xall, dyall, mrow, mcol, w_gate[0], w_up[0], w_down[0])
        y_local, dx_local, grad_wg, grad_wu, grad_wd = outs[:5]
        on_b = [jnp.where(is_b, v, jnp.zeros_like(v))[None] for v in (y_local, grad_wg, grad_wu, grad_wd)]
        dx_local = jnp.where(is_b, jnp.zeros_like(dx_local), dx_local)
        return on_b[0], dx_local[None], on_b[1], on_b[2], on_b[3]

    return jax.shard_map(device_fn, mesh=mesh, in_specs=(tok_spec, tok_spec, tok_spec, w_spec, w_spec, w_spec, tok_spec), out_specs=(tok_spec, tok_spec, w_spec, w_spec, w_spec), check_vma=False)
```

time: 724 us -> 590 us (0.81)
  Pallas kernels: 703 us -> 568 us
    pallas_call x2, Pallas kernels: 703 us -> 568 us  [the longest x1 405 us: device_fn(): pl.pallas_call(functools.partial(main_kernel, n_half, cap), out_shape=(sd...]
where the time goes in v2:
time: 590 us; the launch traced here: 588 us
  Pallas kernels  568 us (96%)
  other arithmetic  12.9 us (2%)
  local copies, waits for them, and re-layouts  6.21 us (1%)
    pallas_call x1, Pallas kernels, device_fn(): pl.pallas_call(functools.partial(main_kernel, n_half, cap), out_shape=(sd...  405 us
    pallas_call x1, Pallas kernels, device_fn(): pl.pallas_call(functools.partial(gather_kernel, n_half, n_part), out_shap...  162 us

profile of v2, /device:TPU:25, one launch (start us, length us, event | category | flops | bytes accessed | tf_op | source)
XLA Modules:
  0.0 587.7 jit_solution(513112654779107493)
XLA Ops:
  0.6 1.8 select_reduce_fusion.g_ref
  2.4 162.1 %gather_tokens.1 = (bf16[8192,1024]{1,0:T(8,128)(2,1)}, bf16[8192,1024]{1,0:T(8,128)(2,1)}, f32[8,32,1024]{2,1,0:T(8,128)}) custom-call(bf16[1024,1024]{1,0:T(8,128)(2,1)} %bitcast.35, bf16[1024,1024]{1,0:T(8,128)(2,1)} %bitcast.36, f32[32,1024]{1,0:T(8,128)} %select_reduce_fusion.g_ref), custom_call_target="tpu_custom_call" | custom-call | tf_op jit(solution)/shard_map/gather_tokens/pallas_call | solution.py:501
  164.5 1.0 constant_dynamic-slice_fusion
  165.5 0.4 fusion.6
  165.9 0.8 fusion.12
  166.6 2.7 copy.17
  169.3 405.5 %experts.1 = (bf16[1024,1024]{1,0:T(8,128)(2,1)}, bf16[1024,1024]{1,0:T(8,128)(2,1)}, bf16[4,1024,512]{2,1,0:T(8,128)(2,1)}, bf16[4,1024,512]{2,1,0:T(8,128)(2,1...) custom-call(bf16[8192,1024]{1,0:T(8,128)(2,1)} %get-tuple-element.13, ...), custom_call_target="tpu_custom_call" | custom-call | tf_op jit(solution)/shard_map/experts/pallas_call | solution.py:519
  574.8 0.0 copy-start.2
  574.8 4.0 select_bitcast_fusion.3
  578.8 0.0 copy-done.2
  578.8 0.0 copy-start
  578.8 0.0 copy-start.1
  578.8 2.4 select_bitcast_fusion
  581.2 1.3 copy-done
  582.5 1.3 copy-done.1
  583.8 3.9 select_bitcast_fusion.1
Async XLA Ops:
  574.8 4.1 copy-start.2
  578.8 3.7 copy-start
  578.8 5.0 copy-start.1

commit v3 on v2

--- a/solution.py
+++ b/solution.py
@@ -137,9 +137,13 @@
             x_arrived(part)
             own(0, part)
 
-        plan = ((relay, 1, 0), (relay, 1, 1), (own_x, 0), (relay, 1, 2), (relay, 1, 3), (diag, 1, 0), (diag, 1, 1), (own_x, 1),
-                (relay, 0, 0), (diag, 1, 2), (diag, 1, 3), (own_x, 2), (relay, 0, 1), (diag, 0, 0), (own_x, 3), (relay, 0, 2),
-                (diag, 0, 1), (relay, 0, 3), (diag, 0, 2), (diag, 0, 3))
+        plan = []
+        for part in range(n_part):
+            at = (part + 1) / n_part
+            x_at = max(100 * at, 67) + 15
+            plan += [(45 * at, relay, 1, part), (50 + 22 * at, diag, 1, part), (100 * at, own_x, part),
+                     (x_at, relay, 0, part), (x_at + 12, diag, 0, part)]
+        plan = [item[1:] for item in sorted(plan, key=lambda item: item[0])]
         for act, *where in plan:
             act(*where)
         for arr_id in range(2):
@@ -158,8 +162,8 @@
 
 
 def main_kernel(n_half, cap, xall, dyall, mrow, mcol, w1, w3, w2, y_out, dx_out, dw1, dw3, dw2, xbuf, qbuf, hbuf, dabuf, dbbuf, sbuf, rbuf,
-                w1v, w3v, w2v, xv, dyv, rv, cv, acc, prv, call, ptv, xs, qs, hs, tv, a1, a3, a2,
-                w_sem, in_sem, st_sem, acc_sem, pr_sem, send_sem, recv_sem, t_sem, o_sem, dx_send, dx_recv, y_sem):
+                w1v, w3v, w2v, xv, dyv, rv, cv, cw, acc, prv, call, ptv, xs, qs, hs, tv, a1, a3, a2,
+                w_sem, in_sem, cw_sem, st_sem, acc_sem, pr_sem, send_sem, recv_sem, t_sem, o_sem, dx_send, dx_recv, y_sem):
     st = lax.axis_index("stage")
     ex = lax.axis_index("expert")
     n_loc, d_model, d_ff = w1v.shape
@@ -209,8 +213,8 @@
             return [pltpu.make_async_copy(xall.at[block_rows(k)], xv.at[slot], in_sem.at[slot, 0]),
                     pltpu.make_async_copy(dyall.at[block_rows(k)], dyv.at[slot], in_sem.at[slot, 1]), col_load(k)]
 
-        def pick(slot, half, e):
-            rank = cv[slot, half * tile:(half + 1) * tile, e:e + 1]
+        def pick(meta, slot, half, e):
+            rank = meta[slot, half * tile:(half + 1) * tile, e:e + 1]
             return jnp.where(rank == lax.broadcasted_iota(jnp.int32, (tile, cap), 1).astype(F32), 1.0, 0.0).astype(BF16)
 
         def stores(k, e, buf):
@@ -254,32 +258,18 @@
             @pl.when(mask % 2 == 0)
             def _():
                 add_arrived(p, (mask // 2) * 2 + half, half)
-            if p == 0:
-                @pl.when(mask == (2 if half else 4))
+            @pl.when(mask == (2 if half else 4))
+            def _():
+                add_arrived(p, 12 + half, half)
+            acc_save(p, k, half).start()
+
+        def send(p, k):
+            for half in range(2):
+                acc_save(p, k, half).wait()
+
+                @pl.when(k < n_blk - 1)
                 def _():
-                    add_arrived(p, 12 + half, half)
-            acc_save(p, k, half).start()
-
-        def send_previous(p, k):
-            @pl.when(k > 0)
-            def _():
-                for half in range(2):
-                    acc_save(p, k - 1, half).wait()
-                    ready = k < n_blk if p == 0 else k != (6 if half else 4)
-
-                    @pl.when(ready)
-                    def _():
-                        rs_copy(p, k - 1, half).start()
-
-        def merge(half):
-            k = 7 - (2 if half else 4)
-            c = pltpu.make_async_copy(sbuf.at[1, k, half], acc.at[half], acc_sem.at[half])
-            c.start()
-            c.wait()
-            add_arrived(1, 12 + half, half)
-            acc_save(1, k, half).start()
-            acc_save(1, k, half).wait()
-            rs_copy(1, k, half).start()
+                    rs_copy(p, k, half).start()
 
         def finalize(p):
             for half in range(2):
@@ -295,7 +285,7 @@
         for c in w_loads:
             c.wait()
 
-        def step_one(k, _):
+        def step_one(first, k):
             slot = k % 2
             blk = flip(ex, 7 - k)
 
@@ -303,7 +293,6 @@
             def _():
                 for c in x_loads(k + 1):
                     c.start()
-            send_previous(0, k)
             for c in x_loads(k):
                 c.wait()
 
@@ -311,7 +300,7 @@
                 it = k * n_loc + e
                 buf = it % 2
 
-                @pl.when(it >= 2)
+                @pl.when(it >= first * n_loc + 2)
                 def _():
                     for c in stores(k, e, buf):
                         c.wait()
@@ -341,45 +330,66 @@
             lax.fori_loop(0, n_loc, expert, 0)
             for half in range(2):
                 for e in range(n_loc):
-                    ptv[:, e * cap:(e + 1) * cap] = pick(slot, half, e)
+                    ptv[:, e * cap:(e + 1) * cap] = pick(cv, slot, half, e)
                 acc[half] = dot(ptv[...], call[...], 1, 0)
                 finish(0, k, half)
-            return 0
-        lax.fori_loop(0, n_blk, step_one, 0)
-        for half in range(2):
-            acc_save(0, n_blk - 1, half).wait()
-        for buf in range(2):
-            for c in stores(0, 0, buf):
-                c.wait()
 
         def h_loads(k):
             rows = pl.ds(pl.multiple_of(k * cap, cap), cap)
             return [pltpu.make_async_copy(hbuf.at[e, rows], tv.at[k % 2, pl.ds(e * cap, cap)], t_sem.at[k % 2, e])
-                    for e in range(n_loc)] + [col_load(k)]
-
-        for c in h_loads(0):
-            c.start()
-
-        def step_two(k, _):
+                    for e in range(n_loc)] + [pltpu.make_async_copy(mcol.at[block_rows(k)], cw.at[k % 2], cw_sem.at[k % 2])]
+
+        def step_two(last, k):
             slot = k % 2
 
-            @pl.when(k + 1 < n_blk)
+            @pl.when(k + 1 < last)
             def _():
                 for c in h_loads(k + 1):
                     c.start()
-            send_previous(1, k)
             for c in h_loads(k):
                 c.wait()
             for e in range(n_loc):
                 out = dot(tv[slot, e * cap:(e + 1) * cap, :], w2v[e], 1, 0).astype(BF16)
                 for half in range(2):
-                    gate = cv[slot, half * tile:(half + 1) * tile, n_loc + e:n_loc + e + 1]
-                    part = gate * dot(pick(slot, half, e), out, 1, 0)
+                    gate = cw[slot, half * tile:(half + 1) * tile, n_loc + e:n_loc + e + 1]
+                    part = gate * dot(pick(cw, slot, half, e), out, 1, 0)
                     acc[half] = part if e == 0 else acc[half] + part
             for half in range(2):
                 finish(1, k, half)
+
+        last_one = n_blk + 2
+        n_steps = 2 * n_blk
+
+        def plan_of(t):
+            early = t < 4
+            two = jnp.where(early, t // 2, jnp.where(t < last_one, 0, 1))
+            k = jnp.where(early, t % 2, jnp.where(t < last_one, t - 2, t - n_blk))
+            return two, k
+
+        def step(t, _):
+            two, k = plan_of(t)
+
+            @pl.when(t > 0)
+            def _():
+                send(*plan_of(t - 1))
+
+            @pl.when(two == 0)
+            def _():
+                step_one(jnp.where(t < 4, 0, 2), k)
+
+            @pl.when((t == 2) | (t == last_one))
+            def _():
+                for buf in range(2):
+                    for c in stores(0, 0, buf):
+                        c.wait()
+                for c in h_loads(k):
+                    c.start()
+
+            @pl.when(two == 1)
+            def _():
+                step_two(jnp.where(t < 4, 2, n_blk), k)
             return 0
-        lax.fori_loop(0, n_blk, step_two, 0)
+        lax.fori_loop(0, n_steps, step, 0)
         for half in range(2):
             acc_save(1, n_blk - 1, half).wait()
 
@@ -414,19 +424,12 @@
                 for c in d_loads(it + 1):
                     c.start()
 
-            @pl.when(it == 2)
+            @pl.when(it == 1)
             def _():
                 finalize(0)
                 for half in range(2):
                     dx_copy(half).start()
 
-            @pl.when(it == 8)
-            def _():
-                merge(1)
-
-            @pl.when(it == 12)
-            def _():
-                merge(0)
             for c in d_loads(it):
                 c.wait()
 
@@ -529,10 +532,11 @@
             scratch_shapes=[
                 vm((n_loc, d_model, d_ff), BF16), vm((n_loc, d_model, d_ff), BF16), vm((n_loc, d_ff, d_model), BF16),
                 vm((2, tok, d_model), BF16), vm((2, tok, d_model), BF16), vm((n_group, 2 * n_loc, tok), F32), vm((2, tok, 2 * n_loc), F32),
+                vm((2, tok, 2 * n_loc), F32),
                 vm((2, tile, d_model), F32), vm((tile, d_model), F32), vm((n_loc * cap, d_model), BF16), vm((tile, n_loc * cap), BF16),
                 vm((2 * cap, d_model), BF16), vm((2 * cap, d_model), BF16), vm((6 * cap, d_ff), BF16), vm((2, 6 * cap, d_ff), BF16),
                 vm((d_model, d_ff), F32), vm((d_model, d_ff), F32), vm((d_ff, d_model), F32),
-                dma((4,)), dma((2, 3)), dma((2, 5)), dma((2,)), dma, dma((2, 14)), dma((2, 14)),
+                dma((4,)), dma((2, 3)), dma((2,)), dma((2, 5)), dma((2,)), dma, dma((2, 14)), dma((2, 14)),
                 dma((2, n_loc)), dma((3,)), dma((2,)), dma((2,)), dma((2,))],
             compiler_params=pltpu.CompilerParams(collective_id=1, has_side_effects=True, vmem_limit_bytes=63 * 1024 * 1024),
             name="experts",

time: 590 us -> 594 us (level)
  the two profiles are of different devices: /device:TPU:25 before, /device:TPU:16 now
where the time goes in v3:
time: 594 us; the launch traced here: 592 us
  Pallas kernels  572 us (96%)
  other arithmetic  12.9 us (2%)
  local copies, waits for them, and re-layouts  6.21 us (1%)
    pallas_call x1, Pallas kernels, device_fn(): pl.pallas_call(functools.partial(main_kernel, n_half, cap), out_shape=(sd...  407 us
    pallas_call x1, Pallas kernels, device_fn(): pl.pallas_call(functools.partial(gather_kernel, n_half, n_part), out_shap...  165 us

profile of v3, /device:TPU:16, one launch (start us, length us, event | category | flops | bytes accessed | tf_op | source)
XLA Modules:
  0.0 592.5 jit_solution(3047629069782992477)
XLA Ops:
  0.6 1.8 select_reduce_fusion.g_ref
  2.4 165.1 %gather_tokens.1 = (bf16[8192,1024]{1,0:T(8,128)(2,1)}, bf16[8192,1024]{1,0:T(8,128)(2,1)}, f32[8,32,1024]{2,1,0:T(8,128)}) custom-call(bf16[1024,1024]{1,0:T(8,128)(2,1)} %bitcast.35, bf16[1024,1024]{1,0:T(8,128)(2,1)} %bitcast.36, f32[32,1024]{1,0:T(8,128)} %select_reduce_fusion.g_ref), custom_call_target="tpu_custom_call" | custom-call | tf_op jit(solution)/shard_map/gather_tokens/pallas_call | solution.py:504
  167.5 1.0 constant_dynamic-slice_fusion
  168.5 0.4 fusion.6
  168.9 0.8 fusion.12
  169.7 2.7 copy.17
  172.3 407.2 %experts.1 = (bf16[1024,1024]{1,0:T(8,128)(2,1)}, bf16[1024,1024]{1,0:T(8,128)(2,1)}, bf16[4,1024,512]{2,1,0:T(8,128)(2,1)}, bf16[4,1024,512]{2,1,0:T(8,128)(2,1...) custom-call(bf16[8192,1024]{1,0:T(8,128)(2,1)} %get-tuple-element.13, ...), custom_call_target="tpu_custom_call" | custom-call | tf_op jit(solution)/shard_map/experts/pallas_call | solution.py:522
  579.5 0.0 copy-start.2
  579.5 4.0 select_bitcast_fusion.3
  583.6 0.0 copy-done.2
  583.6 0.0 copy-start
  583.6 0.0 copy-start.1
  583.6 2.4 select_bitcast_fusion
  586.0 1.3 copy-done
  587.3 1.3 copy-done.1
  588.5 3.9 select_bitcast_fusion.1
Async XLA Ops:
  579.5 4.1 copy-start.2
  583.6 3.7 copy-start
  583.6 5.0 copy-start.1

commit v4 on v3

--- a/solution.py
+++ b/solution.py
@@ -137,13 +137,9 @@
             x_arrived(part)
             own(0, part)
 
-        plan = []
-        for part in range(n_part):
-            at = (part + 1) / n_part
-            x_at = max(100 * at, 67) + 15
-            plan += [(45 * at, relay, 1, part), (50 + 22 * at, diag, 1, part), (100 * at, own_x, part),
-                     (x_at, relay, 0, part), (x_at + 12, diag, 0, part)]
-        plan = [item[1:] for item in sorted(plan, key=lambda item: item[0])]
+        plan = ((relay, 1, 0), (relay, 1, 1), (own_x, 0), (relay, 1, 2), (relay, 1, 3), (diag, 1, 0), (diag, 1, 1), (own_x, 1),
+                (relay, 0, 0), (diag, 1, 2), (diag, 1, 3), (own_x, 2), (relay, 0, 1), (diag, 0, 0), (own_x, 3), (relay, 0, 2),
+                (diag, 0, 1), (relay, 0, 3), (diag, 0, 2), (diag, 0, 3))
         for act, *where in plan:
             act(*where)
         for arr_id in range(2):
@@ -271,14 +267,17 @@
                 def _():
                     rs_copy(p, k, half).start()
 
-        def finalize(p):
-            for half in range(2):
-                c = pltpu.make_async_copy(sbuf.at[p, 7, half], acc.at[half], acc_sem.at[half])
-                c.start()
-                c.wait()
-                for mask in (4, 2):
-                    add_arrived(p, 6 + mask + half, half)
-                call[half * tile:(half + 1) * tile, :] = acc[half].astype(BF16)
+        def finalize(p, half, out):
+            c = pltpu.make_async_copy(sbuf.at[p, 7, half], acc.at[half], acc_sem.at[half])
+            c.start()
+            c.wait()
+            for mask in (4, 2):
+                add_arrived(p, 6 + mask + half, half)
+            out[...] = acc[half].astype(BF16)
+
+        def finish_dx(half):
+            finalize(0, half, out_rows(half))
+            dx_copy(half).start()
 
         for c in x_loads(0):
             c.start()
@@ -373,6 +372,10 @@
             def _():
                 send(*plan_of(t - 1))
 
+            @pl.when(t == last_one + 1)
+            def _():
+                finish_dx(0)
+
             @pl.when(two == 0)
             def _():
                 step_one(jnp.where(t < 4, 0, 2), k)
@@ -426,9 +429,7 @@
 
             @pl.when(it == 1)
             def _():
-                finalize(0)
-                for half in range(2):
-                    dx_copy(half).start()
+                finish_dx(1)
 
             for c in d_loads(it):
                 c.wait()
@@ -457,14 +458,15 @@
             return 0
         lax.fori_loop(0, total, step_three, 0)
 
+        y_rows = (xs.at[pl.ds(0, tile)], call.at[pl.ds(2 * tile, tile)])
+
+        def y_save(half):
+            return pltpu.make_async_copy(y_rows[half], y_out.at[pl.ds(half * tile, tile)], y_sem.at[half])
+        for half in range(2):
+            finalize(1, half, y_rows[half])
+            y_save(half).start()
         for half in range(2):
             dx_copy(half).wait_send()
-        finalize(1)
-
-        def y_save(half):
-            return pltpu.make_async_copy(out_rows(half), y_out.at[pl.ds(half * tile, tile)], y_sem.at[half])
-        for half in range(2):
-            y_save(half).start()
         for half in range(2):
             y_save(half).wait()
         for c in w_saves(n_loc - 1):

time: 594 us -> 548 us (0.923)
  the two profiles are of different devices: /device:TPU:16 before, /device:TPU:25 now
where the time goes in v4:
time: 548 us; the launch traced here: 547 us
  Pallas kernels  527 us (96%)
  other arithmetic  12.9 us (2%)
  local copies, waits for them, and re-layouts  6.21 us (1%)
    pallas_call x1, Pallas kernels, device_fn(): pl.pallas_call(functools.partial(main_kernel, n_half, cap), out_shape=(sd...  365 us
    pallas_call x1, Pallas kernels, device_fn(): pl.pallas_call(functools.partial(gather_kernel, n_half, n_part), out_shap...  162 us

profile of v4, /device:TPU:25, one launch (start us, length us, event | category | flops | bytes accessed | tf_op | source)
XLA Modules:
  0.0 546.8 jit_solution(5606471337489382354)
XLA Ops:
  0.6 1.8 select_reduce_fusion.g_ref
  2.4 162.1 %gather_tokens.1 = (bf16[8192,1024]{1,0:T(8,128)(2,1)}, bf16[8192,1024]{1,0:T(8,128)(2,1)}, f32[8,32,1024]{2,1,0:T(8,128)}) custom-call(bf16[1024,1024]{1,0:T(8,128)(2,1)} %bitcast.35, bf16[1024,1024]{1,0:T(8,128)(2,1)} %bitcast.36, f32[32,1024]{1,0:T(8,128)} %select_reduce_fusion.g_ref), custom_call_target="tpu_custom_call" | custom-call | tf_op jit(solution)/shard_map/gather_tokens/pallas_call | solution.py:506
  164.5 1.0 constant_dynamic-slice_fusion
  165.5 0.4 fusion.6
  165.9 0.8 fusion.12
  166.6 2.7 copy.17
  169.3 364.5 %experts.1 = (bf16[1024,1024]{1,0:T(8,128)(2,1)}, bf16[1024,1024]{1,0:T(8,128)(2,1)}, bf16[4,1024,512]{2,1,0:T(8,128)(2,1)}, bf16[4,1024,512]{2,1,0:T(8,128)(2,1...) custom-call(bf16[8192,1024]{1,0:T(8,128)(2,1)} %get-tuple-element.13, ...), custom_call_target="tpu_custom_call" | custom-call | tf_op jit(solution)/shard_map/experts/pallas_call | solution.py:524
  533.8 0.0 copy-start.2
  533.8 4.0 select_bitcast_fusion.3
  537.9 0.0 copy-done.2
  537.9 0.0 copy-start
  537.9 0.0 copy-start.1
  537.9 2.4 select_bitcast_fusion
  540.3 1.3 copy-done
  541.6 1.3 copy-done.1
  542.8 3.9 select_bitcast_fusion.1
Async XLA Ops:
  533.8 4.1 copy-start.2
  537.9 3.7 copy-start
  537.9 5.0 copy-start.1

commit v5 on v4

--- a/solution.py
+++ b/solution.py
@@ -230,21 +230,33 @@
                 src_ref=sbuf.at[p, k, half], dst_ref=rbuf.at[p, slot], send_sem=send_sem.at[p, slot], recv_sem=recv_sem.at[p, slot],
                 device_id=(st, flip(ex, hop)), device_id_type=MESH)
 
-        def add_arrived(p, slot, dst):
+        def load_of(p, slot, buf):
+            return pltpu.make_async_copy(rbuf.at[p, slot], prv.at[buf], pr_sem.at[buf])
+
+        def fetch(p, slot, buf):
             view = rbuf.at[p, slot]
             pltpu.make_async_remote_copy(
                 src_ref=view, dst_ref=view, send_sem=send_sem.at[p, slot], recv_sem=recv_sem.at[p, slot],
                 device_id=(st, flip(ex, 1)), device_id_type=MESH).wait_recv()
-            c = pltpu.make_async_copy(view, prv, pr_sem)
-            c.start()
-            c.wait()
+            load_of(p, slot, buf).start()
+
+        def add_fetched(p, slot, half):
+            load_of(p, slot, half).wait()
 
             def add(i, _):
                 rows = pl.ds(pl.multiple_of(i * 64, 64), 64)
-                acc[dst, rows] = acc[dst, rows] + prv[rows]
+                acc[half, rows] = acc[half, rows] + prv[half, rows]
                 return 0
             lax.fori_loop(0, tile // 64, add, 0)
 
+        def fetch_partner(p, k):
+            mask = 7 - k
+
+            @pl.when(mask % 2 == 0)
+            def _():
+                for half in range(2):
+                    fetch(p, (mask // 2) * 2 + half, half)
+
         def acc_save(p, k, half):
             return pltpu.make_async_copy(acc.at[half], sbuf.at[p, k, half], acc_sem.at[half])
 
@@ -253,14 +265,17 @@
 
             @pl.when(mask % 2 == 0)
             def _():
-                add_arrived(p, (mask // 2) * 2 + half, half)
+                add_fetched(p, (mask // 2) * 2 + half, half)
             @pl.when(mask == (2 if half else 4))
             def _():
-                add_arrived(p, 12 + half, half)
+                fetch(p, 12 + half, half)
+                add_fetched(p, 12 + half, half)
             acc_save(p, k, half).start()
 
-        def send(p, k):
-            for half in range(2):
+        def send(t, half):
+            @pl.when(t > 0)
+            def _():
+                p, k = plan_of(t - 1)
                 acc_save(p, k, half).wait()
 
                 @pl.when(k < n_blk - 1)
@@ -270,10 +285,18 @@
         def finalize(p, half, out):
             c = pltpu.make_async_copy(sbuf.at[p, 7, half], acc.at[half], acc_sem.at[half])
             c.start()
+            slots = (10 + half, 8 + half)
+            for buf, slot in enumerate(slots):
+                fetch(p, slot, buf)
             c.wait()
-            for mask in (4, 2):
-                add_arrived(p, 6 + mask + half, half)
-            out[...] = acc[half].astype(BF16)
+            for buf, slot in enumerate(slots):
+                load_of(p, slot, buf).wait()
+
+            def add(i, _):
+                rows = pl.ds(pl.multiple_of(i * 64, 64), 64)
+                out[rows, :] = (acc[half, rows] + prv[0, rows] + prv[1, rows]).astype(BF16)
+                return 0
+            lax.fori_loop(0, tile // 64, add, 0)
 
         def finish_dx(half):
             finalize(0, half, out_rows(half))
@@ -284,7 +307,7 @@
         for c in w_loads:
             c.wait()
 
-        def step_one(first, k):
+        def step_one(t, first, k):
             slot = k % 2
             blk = flip(ex, 7 - k)
 
@@ -298,6 +321,10 @@
             def expert(e, _):
                 it = k * n_loc + e
                 buf = it % 2
+
+                @pl.when(e == 1)
+                def _():
+                    send(t, 1)
 
                 @pl.when(it >= first * n_loc + 2)
                 def _():
@@ -327,6 +354,7 @@
                     c.start()
                 return 0
             lax.fori_loop(0, n_loc, expert, 0)
+            fetch_partner(0, k)
             for half in range(2):
                 for e in range(n_loc):
                     ptv[:, e * cap:(e + 1) * cap] = pick(cv, slot, half, e)
@@ -338,7 +366,7 @@
             return [pltpu.make_async_copy(hbuf.at[e, rows], tv.at[k % 2, pl.ds(e * cap, cap)], t_sem.at[k % 2, e])
                     for e in range(n_loc)] + [pltpu.make_async_copy(mcol.at[block_rows(k)], cw.at[k % 2], cw_sem.at[k % 2])]
 
-        def step_two(last, k):
+        def step_two(t, last, k):
             slot = k % 2
 
             @pl.when(k + 1 < last)
@@ -349,6 +377,10 @@
                 c.wait()
             for e in range(n_loc):
                 out = dot(tv[slot, e * cap:(e + 1) * cap, :], w2v[e], 1, 0).astype(BF16)
+                if e == 0:
+                    send(t, 1)
+                if e == n_loc - 1:
+                    fetch_partner(1, k)
                 for half in range(2):
                     gate = cw[slot, half * tile:(half + 1) * tile, n_loc + e:n_loc + e + 1]
                     part = gate * dot(pick(cw, slot, half, e), out, 1, 0)
@@ -368,9 +400,7 @@
         def step(t, _):
             two, k = plan_of(t)
 
-            @pl.when(t > 0)
-            def _():
-                send(*plan_of(t - 1))
+            send(t, 0)
 
             @pl.when(t == last_one + 1)
             def _():
@@ -378,7 +408,7 @@
 
             @pl.when(two == 0)
             def _():
-                step_one(jnp.where(t < 4, 0, 2), k)
+                step_one(t, jnp.where(t < 4, 0, 2), k)
 
             @pl.when((t == 2) | (t == last_one))
             def _():
@@ -390,7 +420,7 @@
 
             @pl.when(two == 1)
             def _():
-                step_two(jnp.where(t < 4, 2, n_blk), k)
+                step_two(t, jnp.where(t < 4, 2, n_blk), k)
             return 0
         lax.fori_loop(0, n_steps, step, 0)
         for half in range(2):
@@ -535,10 +565,10 @@
                 vm((n_loc, d_model, d_ff), BF16), vm((n_loc, d_model, d_ff), BF16), vm((n_loc, d_ff, d_model), BF16),
                 vm((2, tok, d_model), BF16), vm((2, tok, d_model), BF16), vm((n_group, 2 * n_loc, tok), F32), vm((2, tok, 2 * n_loc), F32),
                 vm((2, tok, 2 * n_loc), F32),
-                vm((2, tile, d_model), F32), vm((tile, d_model), F32), vm((n_loc * cap, d_model), BF16), vm((tile, n_loc * cap), BF16),
+                vm((2, tile, d_model), F32), vm((2, tile, d_model), F32), vm((n_loc * cap, d_model), BF16), vm((tile, n_loc * cap), BF16),
                 vm((2 * cap, d_model), BF16), vm((2 * cap, d_model), BF16), vm((6 * cap, d_ff), BF16), vm((2, 6 * cap, d_ff), BF16),
                 vm((d_model, d_ff), F32), vm((d_model, d_ff), F32), vm((d_ff, d_model), F32),
-                dma((4,)), dma((2, 3)), dma((2,)), dma((2, 5)), dma((2,)), dma, dma((2, 14)), dma((2, 14)),
+                dma((4,)), dma((2, 3)), dma((2,)), dma((2, 5)), dma((2,)), dma((2,)), dma((2, 14)), dma((2, 14)),
                 dma((2, n_loc)), dma((3,)), dma((2,)), dma((2,)), dma((2,))],
             compiler_params=pltpu.CompilerParams(collective_id=1, has_side_effects=True, vmem_limit_bytes=63 * 1024 * 1024),
             name="experts",

time: 548 us -> 524 us (0.956)
  Pallas kernels: 527 us -> 504 us
    pallas_call x1, Pallas kernels: 365 us -> 342 us  [device_fn(): pl.pallas_call(functools.partial(main_kernel, n_half, cap), out_shape=(sd...]
where the time goes in v5:
time: 524 us
  Pallas kernels  504 us (96%)
  other arithmetic  12.9 us (2%)
  local copies, waits for them, and re-layouts  6.21 us (1%)
    pallas_call x1, Pallas kernels, device_fn(): pl.pallas_call(functools.partial(main_kernel, n_half, cap), out_shape=(sd...  342 us
    pallas_call x1, Pallas kernels, device_fn(): pl.pallas_call(functools.partial(gather_kernel, n_half, n_part), out_shap...  162 us

profile of v5, /device:TPU:25, one launch (start us, length us, event | category | flops | bytes accessed | tf_op | source)
XLA Modules:
  0.0 523.9 jit_solution(13229452299644870695)
XLA Ops:
  0.6 1.8 select_reduce_fusion.g_ref
  2.4 162.1 %gather_tokens.1 = (bf16[8192,1024]{1,0:T(8,128)(2,1)}, bf16[8192,1024]{1,0:T(8,128)(2,1)}, f32[8,32,1024]{2,1,0:T(8,128)}) custom-call(bf16[1024,1024]{1,0:T(8,128)(2,1)} %bitcast.35, bf16[1024,1024]{1,0:T(8,128)(2,1)} %bitcast.36, f32[32,1024]{1,0:T(8,128)} %select_reduce_fusion.g_ref), custom_call_target="tpu_custom_call" | custom-call | tf_op jit(solution)/shard_map/gather_tokens/pallas_call | solution.py:536
  164.5 1.0 constant_dynamic-slice_fusion
  165.5 0.4 fusion.6
  165.9 0.8 fusion.12
  166.6 2.7 copy.17
  169.3 341.7 %experts.1 = (bf16[1024,1024]{1,0:T(8,128)(2,1)}, bf16[1024,1024]{1,0:T(8,128)(2,1)}, bf16[4,1024,512]{2,1,0:T(8,128)(2,1)}, bf16[4,1024,512]{2,1,0:T(8,128)(2,1...) custom-call(bf16[8192,1024]{1,0:T(8,128)(2,1)} %get-tuple-element.13, ...), custom_call_target="tpu_custom_call" | custom-call | tf_op jit(solution)/shard_map/experts/pallas_call | solution.py:554
  511.0 0.0 copy-start.2
  511.0 4.0 select_bitcast_fusion.3
  515.0 0.0 copy-done.2
  515.0 0.0 copy-start
  515.0 0.0 copy-start.1
  515.0 2.4 select_bitcast_fusion
  517.4 1.3 copy-done
  518.7 1.3 copy-done.1
  520.0 3.9 select_bitcast_fusion.1
Async XLA Ops:
  511.0 4.1 copy-start.2
  515.0 3.7 copy-start
  515.0 5.0 copy-start.1
